TPU v7x, 256 devices: a whole 4x4x8 slice. The times are simulated.
256 devices in a mesh: enc: 8 (over z), bin: 16 (over y_hi, x, core), off: 2 (over y_lo).
Axes of the slice: x: 4, y: 4 (y_hi: 2, y_lo: 2; y = y_hi * 2 + y_lo), z: 8, core: 2. Of those that a mesh axis runs over, the one named last changes fastest.
Arguments:
- encoder_in: bfloat16 [512, 6144], P(('bin', 'off'), 'enc'), may hold values from -6 to 6
- gain_enc: float32 [512], P(('bin', 'off')), may hold values from 0.1 to 1.9
- conv_one: bfloat16 [3, 512, 512], P(None, ('bin', 'off')), may hold values from -0.15625 to 0.15625
- proj_weight: bfloat16 [2, 512, 32], P(None, ('bin', 'off')), may hold values from -0.25 to 0.25
- conv_two: bfloat16 [9, 32, 32], replicated, may hold values from -0.375 to 0.375
- head_weight: float32 [32], replicated, may hold values from -1 to 1
- target: bfloat16 [6144, 2048], P('bin', ('enc', 'off')), may hold values from -8 to 8
- valid_bins: int32 [6144], replicated, may hold values 0 or 1
- offset_limit: int32 [6144], replicated, may hold values from 1024 to 2048
- dilations: int32 [2], replicated, may hold values from 1 to 8, as said below
Outputs:
- prediction: float32 [6144, 2048], P('bin', ('enc', 'off'))
- loss_mean: float32 [1], replicated
- grad_conv_two: float32 [9, 32, 32], replicated
- grad_proj: float32 [2, 512, 32], P(None, ('bin', 'off'))
- grad_conv_one: float32 [3, 512, 512], P(None, ('bin', 'off'), 'enc')
Inputs may be any that keep to these rules, and one draw needn't show every extreme that they name: dilations[0] is the dilation of the 1-D layer and dilations[1] that of the 2-D layer; one of the two equals 8, the other is smaller.
All inputs are finite; a program needn't handle non-finite values.
Results may differ from a plain program's by a relative error of at most 0.0013.
The roundings to bfloat16 on the way count: a program that leaves them out, or rounds other values in their place, can miss the bound.
Values may be sent and summed in bfloat16 or wider, within the bound.
No kernel may reach another device: no remote copies, remote signals or barrier semaphores. Data moves between devices by JAX's collectives and lax.ppermute only.
A program may use at most 192 MiB of HBM per device.

v0:
```python
import jax
import jax.numpy as jnp
from jax import lax
from jax.sharding import PartitionSpec as P

LARGEST_DILATION = 8


def with_halo(cells, sides, width):
    for axis, dim in sides:
        count = lax.axis_size(axis)
        ends = count - 1
        head = lax.slice_in_dim(cells, 0, width, axis=dim)
        tail = lax.slice_in_dim(cells, cells.shape[dim] - width, cells.shape[dim], axis=dim)
        cells = jnp.concatenate(
            [
                lax.ppermute(tail, axis, [(i, (i + 1) % count) for i in range(ends)]),
                cells,
                lax.ppermute(head, axis, [((i + 1) % count, i) for i in range(ends)]),
            ],
            axis=dim,
        )
    return cells


def from_everyone(array, axis):
    size = lax.axis_size(axis)
    return lax.all_to_all(
        jnp.broadcast_to(array[None], (size, *array.shape)), axis, 0, 0, tiled=True
    )


def laid_out(tiles, dim):
    tiles = jnp.moveaxis(tiles, 0, dim)
    shape = tiles.shape
    return tiles.reshape(*shape[:dim], shape[dim] * shape[dim + 1], *shape[dim + 2 :])


def gathered_copies(array, axis, dim):
    tiles = from_everyone(array, axis)
    return laid_out(tiles, dim)


def total_of_pieces(array, axis):
    tiles = lax.all_gather(array, axis)
    return tiles.sum(axis=0)


def of_everyone(array, axis):
    return from_everyone(array, axis).sum(axis=0)


def split_up(array, dim, size):
    shape = array.shape
    tiles = array.reshape(*shape[:dim], size, shape[dim] // size, *shape[dim + 1 :])
    return jnp.moveaxis(tiles, dim, 0)


def sum_at_owner(array, axis, dim):
    size = lax.axis_size(axis)
    tiles = lax.all_to_all(split_up(array, dim, size), axis, 0, 0, tiled=True)
    return jnp.sum(tiles, axis=0)


def hankel(window, tile_rows, tile_cols):
    chans = window.shape[0]
    width = tile_rows + tile_cols
    base = window[:, : width - 1]
    tiled = jnp.broadcast_to(base[:, None, :], (chans, tile_rows, width - 1)).reshape(
        chans, tile_rows * (width - 1)
    )
    tiled = jnp.pad(tiled, ((0, 0), (0, tile_rows)))
    return tiled.reshape(chans, tile_rows, width)[:, :, :tile_cols]


def diagonal_sums(tile):
    chans, tile_rows, tile_cols = tile.shape
    width = tile_rows + tile_cols
    padded_input = jnp.pad(tile, ((0, 0), (0, 0), (0, tile_rows)))
    flat = padded_input.reshape(chans, tile_rows * width)[:, : tile_rows * (width - 1)]
    return jnp.sum(flat.reshape(chans, tile_rows, width - 1), axis=1)


def count_cells(valid_bins, offset_limit):
    sequence_length = valid_bins.shape[0]
    running = jnp.concatenate([jnp.zeros((1,), jnp.int32), jnp.cumsum(valid_bins)])
    places = jnp.arange(sequence_length, dtype=jnp.int32)
    farthest = jnp.minimum(places + offset_limit, sequence_length)
    inside = jnp.take(running, farthest) - jnp.take(running, places)
    return jnp.sum(valid_bins * inside).astype(jnp.float32)


def shards(
    encoder_in,
    gain_enc,
    conv_one,
    proj_weight,
    conv_two,
    head_weight,
    target,
    valid_bins,
    offset_limit,
    dilations,
):
    chans, encoder_bins = encoder_in.shape
    width_in = conv_one.shape[2]
    second_channels = conv_two.shape[1]
    tile_rows, tile_cols = target.shape
    area = tile_rows * tile_cols
    first_dilation = dilations[0]
    second_dilation = dilations[1]
    activ = jax.nn.gelu(gain_enc[:, None] * encoder_in.astype(jnp.float32)).astype(jnp.bfloat16)
    framed = with_halo(activ, (("enc", 1),), LARGEST_DILATION)
    channel_count = gathered_copies(framed, ("bin", "off"), 0)
    stacked_enc = jnp.concatenate(
        [
            lax.dynamic_slice_in_dim(
                channel_count,
                LARGEST_DILATION + (kernel_tap_index - 1) * first_dilation,
                encoder_bins,
                1,
            )
            for kernel_tap_index in range(3)
        ],
        axis=0,
    )
    weight_one = jnp.transpose(conv_one, (1, 0, 2)).reshape(chans, 3 * width_in)
    conv_out = jnp.dot(weight_one, stacked_enc, preferred_element_type=jnp.float32)
    hidden = (encoder_in.astype(jnp.float32) + conv_out).astype(jnp.bfloat16)
    proj_rows = jnp.transpose(proj_weight, (0, 2, 1)).reshape(2 * second_channels, chans)
    partial_embed = jnp.dot(proj_rows, hidden, preferred_element_type=jnp.float32)
    summed = total_of_pieces(partial_embed, ("bin", "off")).astype(jnp.bfloat16)
    embed = gathered_copies(summed, "enc", 1)
    sequence_length = embed.shape[1]
    window_extent = tile_cols * lax.axis_size("enc") * lax.axis_size("off")
    row_start = lax.axis_index("bin") * tile_rows
    offs_start = (lax.axis_index("enc") * lax.axis_size("off") + lax.axis_index("off")) * tile_cols
    near_rows = lax.dynamic_slice_in_dim(embed[:second_channels], row_start, tile_rows, 1)
    far_ext = jnp.concatenate(
        [embed[second_channels:], jnp.zeros((second_channels, window_extent), jnp.bfloat16)], axis=1
    )
    far_window = lax.dynamic_slice_in_dim(far_ext, row_start + offs_start, tile_rows + tile_cols, 1)
    pair_sum = near_rows[:, :, None].astype(jnp.float32) + hankel(
        far_window, tile_rows, tile_cols
    ).astype(jnp.float32)
    band_act = jnp.maximum(pair_sum, 0.0).astype(jnp.bfloat16)
    shifts = [
        (bin_displacement, offset_displacement)
        for bin_displacement in (-1, 0, 1)
        for offset_displacement in (-1, 0, 1)
    ]
    framed_band = with_halo(band_act, (("bin", 1), (("enc", "off"), 2)), LARGEST_DILATION)
    stacked_band = jnp.concatenate(
        [
            lax.dynamic_slice(
                framed_band,
                (
                    0,
                    LARGEST_DILATION + bin_displacement * second_dilation,
                    LARGEST_DILATION + offset_displacement * second_dilation,
                ),
                (second_channels, tile_rows, tile_cols),
            ).reshape(second_channels, area)
            for bin_displacement, offset_displacement in shifts
        ],
        axis=0,
    )
    weight_fwd = jnp.transpose(conv_two, (2, 0, 1)).reshape(second_channels, 9 * second_channels)
    band_conv = jnp.dot(weight_fwd, stacked_band, preferred_element_type=jnp.float32).reshape(
        second_channels, tile_rows, tile_cols
    )
    resid = pair_sum + band_conv
    prediction = jnp.sum(head_weight[:, None, None] * jnp.maximum(resid, 0.0), axis=0)
    mask_float = valid_bins.astype(jnp.float32)
    mask_ext = jnp.concatenate([mask_float, jnp.zeros((window_extent,), jnp.float32)])
    mask_near = lax.dynamic_slice_in_dim(mask_float, row_start, tile_rows)
    mask_far = hankel(
        lax.dynamic_slice_in_dim(mask_ext, row_start + offs_start, tile_rows + tile_cols)[None, :],
        tile_rows,
        tile_cols,
    )[0]
    limit_near = lax.dynamic_slice_in_dim(offset_limit, row_start, tile_rows)
    offs_ids = offs_start + jnp.arange(tile_cols, dtype=jnp.int32)
    weight = (
        mask_near[:, None]
        * mask_far
        * (offs_ids[None, :] < limit_near[:, None]).astype(jnp.float32)
    )
    denom = 1.0 + count_cells(valid_bins, offset_limit)
    differ = prediction - target.astype(jnp.float32)
    error_sum = jnp.sum(weight * differ * differ)
    dpred = 2.0 * weight * differ / denom
    dres = (head_weight[:, None, None] * dpred[None] * (resid > 0.0).astype(jnp.float32)).astype(
        jnp.bfloat16
    )
    grad_band = lax.dot_general(
        stacked_band,
        dres.reshape(second_channels, area),
        (((1,), (1,)), ((), ())),
        preferred_element_type=jnp.float32,
    ).reshape(9, second_channels, second_channels)
    framed_grad = with_halo(dres, (("bin", 1), (("enc", "off"), 2)), LARGEST_DILATION)
    stacked_grad = jnp.concatenate(
        [
            lax.dynamic_slice(
                framed_grad,
                (
                    0,
                    LARGEST_DILATION - bin_displacement * second_dilation,
                    LARGEST_DILATION - offset_displacement * second_dilation,
                ),
                (second_channels, tile_rows, tile_cols),
            ).reshape(second_channels, area)
            for bin_displacement, offset_displacement in shifts
        ],
        axis=0,
    )
    weight_back = jnp.transpose(conv_two, (1, 0, 2)).reshape(second_channels, 9 * second_channels)
    dact = jnp.dot(weight_back, stacked_grad, preferred_element_type=jnp.float32).reshape(
        second_channels, tile_rows, tile_cols
    )
    dpair = dres.astype(jnp.float32) + dact * (pair_sum > 0.0).astype(jnp.float32)
    near_grad = jnp.sum(dpair, axis=2)
    far_grad = diagonal_sums(dpair)
    enc_start = lax.axis_index("enc") * encoder_bins
    buffer = jnp.zeros((2, second_channels, sequence_length + window_extent), jnp.float32)
    buffer = lax.dynamic_update_slice(buffer, near_grad[None], (0, 0, row_start))
    buffer = lax.dynamic_update_slice(buffer, far_grad[None], (1, 0, row_start + offs_start))
    buffer = buffer[:, :, :sequence_length]
    grad_whole, grad_conv_two, total_error = lax.psum(
        (buffer, grad_band, error_sum), ("enc", "bin", "off")
    )
    grad_embed = lax.dynamic_slice_in_dim(grad_whole, enc_start, encoder_bins, 2).astype(
        jnp.bfloat16
    )
    grad_rows = grad_embed.reshape(2 * second_channels, encoder_bins)
    dhidden = jnp.dot(proj_rows.T, grad_rows, preferred_element_type=jnp.float32).astype(
        jnp.bfloat16
    )
    proj_local = jnp.dot(hidden, grad_rows.T, preferred_element_type=jnp.float32)
    proj_local = jnp.transpose(proj_local.reshape(chans, 2, second_channels), (1, 0, 2))
    conv_local = lax.dot_general(
        dhidden, stacked_enc, (((1,), (1,)), ((), ())), preferred_element_type=jnp.float32
    )
    conv_local = jnp.transpose(conv_local.reshape(chans, 3, width_in), (1, 0, 2))
    grad_proj = of_everyone(proj_local, "enc")
    grad_conv_one = sum_at_owner(conv_local, "enc", 2)
    loss_mean = (total_error / denom).reshape(1)
    return (prediction, loss_mean, grad_conv_two, grad_proj, grad_conv_one)


def solution(mesh):
    in_specs = (
        P(("bin", "off"), "enc"),
        P(("bin", "off")),
        P(None, ("bin", "off"), None),
        P(None, ("bin", "off"), None),
        P(),
        P(),
        P("bin", ("enc", "off")),
        P(),
        P(),
        P(),
    )
    out_specs = (
        P("bin", ("enc", "off")),
        P(),
        P(),
        P(None, ("bin", "off"), None),
        P(None, ("bin", "off"), "enc"),
    )
    return jax.shard_map(shards, mesh=mesh, in_specs=in_specs, out_specs=out_specs, check_vma=False)
```

profile of v0, /device:TPU:2, one launch (start us, length us, event | category | flops | bytes accessed | tf_op | source)
XLA Modules:
  0.0 811.7 jit_solution(11922956676529906253)
XLA Ops:
  9.4 4.5 collective-permute-start
  16.4 7.6 all-to-all-start
  28.9 10.5 %all-to-all-done = bf16[32,16,784]{2,1,0:T(8,128)(2,1)S(1)} async-done(((bf16[32,16,784]{2,1,0:T(8,128)(2,1)}), bf16[32,16,784]{2,1,0:T(8,128)(2,1)S(1)}, u32[]{:S(2)}, u32[]{:S(2)}) %all-to-all-start) | async-done | bytes 802848 | tf_op jit(solution)/shard_map/all_to_all | solution.py:28
  43.6 92.3 %all-gather.3.cloned.1.call-done = f32[2048,768]{1,0:T(8,128)} async-done(((f32[64,768]{1,0:T(8,128)}), f32[2048,768]{1,0:T(8,128)}) %all-gather.3.cloned.1.call-update) | async-done | bytes 6291472 | tf_op jit(solution)/shard_map/all_gather | solution.py:45
  140.0 7.0 all-to-all-start.1
  147.7 34.3 %gather_fusion.1 = s32[6144]{0:T(1024)S(1)} fusion(s32[6145]{0:T(1024)S(1)} %pad_add_fusion, s32[6144]{0:T(1024)S(1)} %get-tuple-element.63), kind=kCustom, calls=%fused_computation.1.clone | custom fusion | bytes 73728 | tf_op jit(solution)/shard_map/jit(_take)/gather | solution.py:89
  182.0 34.3 %gather_fusion = s32[6144]{0:T(1024)S(1)} fusion(s32[6145]{0:T(1024)S(1)} %pad_add_fusion, s32[6144]{0:T(1024)S(1)} %get-tuple-element.64), kind=kCustom, calls=%fused_computation.clone | custom fusion | bytes 73728 | tf_op jit(solution)/shard_map/jit(_take)/gather | solution.py:89
  216.6 5.5 broadcast_in_dim.30
  222.1 21.4 %reshape.201 = bf16[32,196224]{1,0:T(8,128)(2,1)} reshape(bf16[32,384,511]{2,1,0:T(8,128)(2,1)} %broadcast_in_dim.30) | data formatting | bytes 25116672 | tf_op jit(solution)/shard_map/reshape | solution.py:69
  243.4 6.1 pad.14
  249.6 11.2 %copy.122 = bf16[4,8,384,512]{3,2,1,0:T(8,128)(2,1)S(1)} copy(bf16[4,8,384,512]{3,1,2,0:T(8,128)(2,1)S(1)} %bitcast.171) | data formatting | bytes 25165824
  260.8 4.4 copy-done.1
  275.1 3.9 fusion.30
  278.9 4.0 copy.102
  284.4 4.0 copy.101
  288.4 5.2 collective-permute-start.4
  302.0 10.0 %pad_reduce_fusion = f32[196608]{0:T(1024)} fusion(f32[1,196224]{1,0:T(1,128)} %broadcast_in_dim.34), kind=kLoop, calls=%fused_computation.43 | loop fusion | bytes 1571328 | tf_op jit(solution)/shard_map/jit(_pad)/pad | solution.py:72
  318.1 3.6 copy.104
  321.7 3.7 copy.103
  325.4 8.9 %pad_maximum_fusion = bf16[32,400,144]{2,1,0:T(8,128)(2,1)} fusion(bf16[32,400,8]{2,1,0:T(8,128)(2,1)} %copy.104, bf16[32,8,128]{2,1,0:T(8,128)(2,1)S(1)} %collective-permute-done.3, bf16[32,384,128]{2,1,0:T(8,128)(2,1)S(1)} %maximum_convert_fusion, bf16[32,8,128]{2,1,0:T(8,128)(2,1)} %copy-done.24, bf16[32,400,8]{2,1,0:T(8,128)(2,1)} %copy.103), kind=kLoop, calls=%fused_computation.2 | loop fusion | flops 18432000 | bytes 7372800 | tf_op jit(solution)/shard_map/concatenate | solution.py:15
  334.3 37.5 %constant_dynamic-slice_fusion.8 = (bf16[32,384,128]{2,1,0:T(8,128)(2,1)}, bf16[32,384,128]{2,1,0:T(8,128)(2,1)}, bf16[32,384,128]{2,1,0:T(8,128)(2,1)}, bf16[32...) fusion(bf16[32,400,144]{2,1,0:T(8,128)(2,1)} %pad_maximum_fusio, ...), kind=kLoop, calls=%fused_computation.89 | loop fusion | bytes 50331664 | tf_op jit(solution)/shard_map/dynamic_slice | solution.py:155
  371.9 5.5 bitcast_dynamic-update-slice_fusion.17
  394.9 3.7 bitcast_dynamic-update-slice_fusion.11
  405.7 11.8 %convolution_bitcast_fusion.1 = f32[4,8,384,128]{3,1,2,0:T(8,128)S(1)} fusion(bf16[288,49152]{1,0:T(8,128)(2,1)} %bitcast_dynamic-update-slice_fusion.9, bf16[32,288]{0,1:T(8,128)(2,1)S(1)} %bitcast.195), kind=kOutput, calls=%fused_computation.33 | convolution fusion | flops 905969664 | bytes 34621440 | tf_op jit(solution)/shard_map/dot_general | solution.py:169
  421.3 4.1 multiply_reduce_fusion
  427.2 5.2 select_convert_fusion
  443.0 3.9 fusion.29
  446.9 4.0 copy.110
  452.2 4.0 copy.109
  456.1 5.2 collective-permute-start.8
  461.4 14.4 %fusion.35 = f32[9,32,32]{2,1,0:T(8,128)} fusion(bf16[9,32,49152]{2,1,0:T(8,128)(2,1)} %bitcast.26, bf16[32,49152,1]{1,0,2:T(8,128)(2,1)} %reshape.256), kind=kOutput, calls=%fused_computation.110 | convolution fusion | flops 905969664 | bytes 31494144 | tf_op jit(solution)/shard_map/dot_general | solution.py:196
  475.8 3.6 copy.112
  479.4 3.7 copy.111
  483.1 8.9 %pad_maximum_fusion.1 = bf16[32,400,144]{2,1,0:T(8,128)(2,1)} fusion(bf16[32,400,8]{2,1,0:T(8,128)(2,1)} %copy.112, bf16[32,8,128]{2,1,0:T(8,128)(2,1)S(1)} %collective-permute-done.7, bf16[32,384,128]{2,1,0:T(8,128)(2,1)S(1)} %select_convert_fusion, bf16[32,8,128]{2,1,0:T(8,128)(2,1)S(1)} %collective-permute-done.6, bf16[32,400,8]{2,1,0:T(8,128)(2,1)} %copy.111), kind=kLoop, calls=%fused_computation.3 | loop fusion | flops 18432000 | bytes 7372800 | tf_op jit(solution)/shard_map/concatenate | solution.py:15
  492.0 37.3 %constant_dynamic-slice_fusion = (bf16[32,384,128]{2,1,0:T(8,128)(2,1)}, bf16[32,384,128]{2,1,0:T(8,128)(2,1)}, bf16[32,384,128]{2,1,0:T(8,128)(2,1)}, bf16[32,3...) fusion(bf16[32,400,144]{2,1,0:T(8,128)(2,1)} %pad_maximum_fusio, ...), kind=kLoop, calls=%fused_computation.81 | loop fusion | bytes 50331664 | tf_op jit(solution)/shard_map/dynamic_slice | solution.py:205
  529.4 5.5 bitcast_dynamic-update-slice_fusion.8
  552.4 4.0 bitcast_dynamic-update-slice_fusion.2
  563.4 11.8 %convolution_bitcast_fusion = f32[4,8,384,128]{3,1,2,0:T(8,128)S(1)} fusion(bf16[288,49152]{1,0:T(8,128)(2,1)} %bitcast_dynamic-update-slice_fusion, bf16[32,288]{0,1:T(8,128)(2,1)S(1)} %bitcast.197), kind=kOutput, calls=%fused_computation.32 | convolution fusion | flops 905969664 | bytes 34621440 | tf_op jit(solution)/shard_map/dot_general | solution.py:219
  576.4 6.9 fusion.27
  583.2 14.4 %pad.16 = f32[32,384,512]{2,1,0:T(8,128)} pad(f32[32,384,128]{2,1,0:T(8,128)} %get-tuple-element.25, f32[]{:T(128)} %constant.90.clone.1), padding=0_0x0_0x0_384 | pad | bytes 31457284 | tf_op jit(solution)/shard_map/jit(_pad)/pad | solution.py:79
  597.6 21.9 %copy.143 = f32[4,8,384,512]{3,1,2,0:T(8,128)S(1)} copy(f32[4,8,384,512]{3,2,1,0:T(8,128)} %bitcast.164) | data formatting | bytes 50331648
  619.6 8.6 %slice.118 = f32[32,196224]{1,0:T(8,128)} slice(f32[32,196608]{1,0:T(8,128)S(1)} %bitcast.165), slice={[0:32], [0:196224]} | slice | bytes 50233344 | tf_op jit(solution)/shard_map/slice | solution.py:80
  628.2 43.9 %reshape.230 = f32[32,384,511]{2,1,0:T(8,128)} reshape(f32[32,196224]{1,0:T(8,128)} %slice.118) | data formatting | bytes 50233344 | tf_op jit(solution)/shard_map/reshape | solution.py:81
  672.0 10.0 %reduce_sum.77 = f32[32,511]{1,0:T(8,128)S(1)} reduce(f32[32,384,511]{2,1,0:T(8,128)} %reshape.230, f32[]{:T(128)} %constant.90.clone.1), dimensions={1}, to_apply=%region_9.11 | reduce | flops 6262816 | bytes 25182084 | tf_op jit(solution)/shard_map/reduce_sum | solution.py:81
  684.3 91.2 %all-reduce.7 = (f32[]{:T(128)}, f32[9,32,32]{2,1,0:T(8,128)}, bf16[2,32,6144]{2,1,0:T(8,128)(2,1)S(1)}) all-reduce(f32[]{:T(128)} %get-tuple-element.56, f32[9,32,32]{2,1,0:T(8,128)S(1)} %copy-done.25, f32[2,32,6144]{2,1,0:T(8,128)} %slice.119), channel_id=1, replica_groups=mesh['enc'=8,'bin'=16,'off'=2] {'enc','bin','off'}, use_global_device_ids=true, to_apply=%region_3.4 | all-reduce | flops 402433 | bytes 2433032 | tf_op jit(solution)/shard_map/psum | solution.py:230
  776.4 4.8 all-to-all-start.2
  784.6 4.7 all-to-all-done.2
  795.3 6.7 all-to-all-done.3
  (174 shorter events, 118.0 us)
Async XLA Ops:
  7.2 34.4 %copy-start.30 = (bf16[16,768]{1,0:T(8,128)(2,1)S(1)}, bf16[16,768]{1,0:T(8,128)(2,1)}, u32[]{:S(2)}) copy-start(bf16[16,768]{1,0:T(8,128)(2,1)} %param.12) | copy-start | bytes 73732
  8.2 5.8 collective-permute-start.1
  9.4 5.9 collective-permute-start
  16.4 23.1 %all-to-all-start = ((bf16[32,16,784]{2,1,0:T(8,128)(2,1)}), bf16[32,16,784]{2,1,0:T(8,128)(2,1)S(1)}, u32[]{:S(2)}, u32[]{:S(2)}) async-start(bf16[32,16,784]{2,1,0:T(8,128)(2,1)} %broadcast_in_dim.26), calls=%async_computation | async-start | bytes 1835008 | tf_op jit(solution)/shard_map/all_to_all | solution.py:28
  24.0 111.9 %all-gather.3.cloned.1.call-start = ((), (), s32[]{:S(2)}) async-start(), calls=%async_computation.4 | async-start | bytes 6488064 | tf_op jit(solution)/shard_map/all_gather | solution.py:45
  40.7 1.4 copy-start.19
  41.6 105.4 %copy-start.29 = (s32[6144]{0:T(1024)S(1)}, s32[6144]{0:T(1024)}, u32[]{:S(2)}) copy-start(s32[6144]{0:T(1024)} %param.19) | copy-start | bytes 73732
  41.6 106.1 %copy-start.26 = (s32[6144]{0:T(1024)S(1)}, s32[6144]{0:T(1024)}, u32[]{:S(2)}) copy-start(s32[6144]{0:T(1024)} %param.20) | copy-start | bytes 73732
  140.0 76.3 %all-to-all-start.1 = ((bf16[8,64,768]{2,1,0:T(8,128)(2,1)}), bf16[8,64,768]{2,1,0:T(8,128)(2,1)S(1)}, u32[]{:S(2)}, u32[]{:S(2)}) async-start(bf16[8,64,768]{2,1,0:T(8,128)(2,1)} %broadcast_in_dim.27), calls=%async_computation.1 | async-start | bytes 1572864 | tf_op jit(solution)/shard_map/all_to_all | solution.py:28
  260.8 4.5 copy-start.1
  267.2 5.1 collective-permute-start.3
  269.2 5.6 collective-permute-start.2
  274.8 4.1 copy-start.24
  282.9 35.2 %collective-permute-start.5 = (bf16[32,400,8]{1,2,0:T(8,128)(2,1)}, bf16[32,400,8]{1,2,0:T(8,128)(2,1)}, u32[]{:S(2)}, u32[]{:S(2)}) collective-permute-start(bf16[32,400,8]{1,2,0:T(8,128)(2,1)} %copy.102), channel_id=1, source_target_pairs={{1,0},{32,1},{33,32},{64,33},{65,64},{96,65},{97,96},{128,97},{129... | collective-permute-start | bytes 614408 | tf_op jit(solution)/shard_map/ppermute | solution.py:19
  288.4 33.3 %collective-permute-start.4 = (bf16[32,400,8]{1,2,0:T(8,128)(2,1)}, bf16[32,400,8]{1,2,0:T(8,128)(2,1)}, u32[]{:S(2)}, u32[]{:S(2)}) collective-permute-start(bf16[32,400,8]{1,2,0:T(8,128)(2,1)} %copy.101), channel_id=1, source_target_pairs={{0,1},{1,32},{32,33},{33,64},{64,65},{65,96},{96,97},{97,128},{128... | collective-permute-start | bytes 614408 | tf_op jit(solution)/shard_map/ppermute | solution.py:17
  371.9 5.5 copy-start.14
  371.9 9.0 %copy-start.12 = (bf16[32,384,128]{2,1,0:T(8,128)(2,1)S(1)}, bf16[32,384,128]{2,1,0:T(8,128)(2,1)}, u32[]{:S(2)}) copy-start(bf16[32,384,128]{2,1,0:T(8,128)(2,1)} %get-tuple-element.39) | copy-start | bytes 9437188
  377.4 7.1 copy-start.10
  384.4 7.0 copy-start.8
  387.9 7.0 copy-start.6
  391.4 7.2 copy-start.4
  394.9 7.3 copy-start.2
  398.6 7.0 copy-start.22
  417.5 3.9 copy-start.34
  418.6 2.7 copy-start
  421.3 4.3 copy-start.20
  421.3 4.3 copy-start.31
  421.3 4.3 copy-start.32
  421.3 4.3 copy-start.35
  425.5 7.0 copy-start.21
  427.2 12.2 %copy-start.23 = (bf16[9,32,32]{2,1,0:T(8,128)(2,1)S(1)}, bf16[9,32,32]{2,1,0:T(8,128)(2,1)}, u32[]{:S(2)}) copy-start(bf16[9,32,32]{2,1,0:T(8,128)(2,1)} %param.16) | copy-start | bytes 55300
  433.1 9.7 %collective-permute-start.7 = (bf16[32,8,128]{2,1,0:T(8,128)(2,1)}, bf16[32,8,128]{2,1,0:T(8,128)(2,1)S(1)}, u32[]{:S(2)}, u32[]{:S(2)}) collective-permute-start(bf16[32,8,128]{2,1,0:T(8,128)(2,1)} %get-tuple-element.47), channel_id=1, source_target_pairs={{2,0},{4,2},{6,4},{8,6},{10,8},{12,10},{14,12},{16,14},{18,16},{20... | collective-permute-start | bytes 196616 | tf_op jit(solution)/shard_map/ppermute | solution.py:19
  435.0 7.7 collective-permute-start.6
  450.9 24.9 %collective-permute-start.9 = (bf16[32,400,8]{1,2,0:T(8,128)(2,1)}, bf16[32,400,8]{1,2,0:T(8,128)(2,1)}, u32[]{:S(2)}, u32[]{:S(2)}) collective-permute-start(bf16[32,400,8]{1,2,0:T(8,128)(2,1)} %copy.110), channel_id=1, source_target_pairs={{1,0},{32,1},{33,32},{64,33},{65,64},{96,65},{97,96},{128,97},{129... | collective-permute-start | bytes 614408 | tf_op jit(solution)/shard_map/ppermute | solution.py:19
  456.1 23.3 %collective-permute-start.8 = (bf16[32,400,8]{1,2,0:T(8,128)(2,1)}, bf16[32,400,8]{1,2,0:T(8,128)(2,1)}, u32[]{:S(2)}, u32[]{:S(2)}) collective-permute-start(bf16[32,400,8]{1,2,0:T(8,128)(2,1)} %copy.109), channel_id=1, source_target_pairs={{0,1},{1,32},{32,33},{33,64},{64,65},{65,96},{96,97},{97,128},{128... | collective-permute-start | bytes 614408 | tf_op jit(solution)/shard_map/ppermute | solution.py:17
  529.4 5.5 copy-start.15
  529.4 9.0 %copy-start.13 = (bf16[32,384,128]{2,1,0:T(8,128)(2,1)S(1)}, bf16[32,384,128]{2,1,0:T(8,128)(2,1)}, u32[]{:S(2)}) copy-start(bf16[32,384,128]{2,1,0:T(8,128)(2,1)} %get-tuple-element.31) | copy-start | bytes 9437188
  534.9 7.1 copy-start.11
  541.9 7.0 copy-start.9
  545.4 7.0 copy-start.7
  548.9 7.5 copy-start.5
  552.4 7.5 copy-start.3
  672.0 12.2 %copy-start.25 = (f32[9,32,32]{2,1,0:T(8,128)S(1)}, f32[9,32,32]{2,1,0:T(8,128)}, u32[]{:S(2)}) copy-start(f32[9,32,32]{2,1,0:T(8,128)} %fusion.35) | copy-start | bytes 110596
  682.1 93.4 %copy-start.28 = (bf16[16,768]{1,0:T(8,128)(2,1)S(1)}, bf16[16,768]{1,0:T(8,128)(2,1)}, u32[]{:S(2)}) copy-start(bf16[16,768]{1,0:T(8,128)(2,1)} %copy-done.27) | copy-start | bytes 73732
  682.1 99.2 %copy-start.17 = (bf16[512,768]{1,0:T(8,128)(2,1)S(1)}, bf16[512,768]{1,0:T(8,128)(2,1)}, u32[]{:S(2)}) copy-start(bf16[512,768]{1,0:T(8,128)(2,1)} %copy-done.16) | copy-start | bytes 2359300
  682.1 99.1 %copy-start.33 = (bf16[2,16,32]{2,1,0:T(8,128)(2,1)S(1)}, bf16[2,16,32]{2,1,0:T(8,128)(2,1)}, u32[]{:S(2)}) copy-start(bf16[2,16,32]{2,1,0:T(8,128)(2,1)} %param.15) | copy-start | bytes 6148
  776.4 12.9 %all-to-all-start.2 = ((f32[8,1,1024]{2,1,0:T(1,128)}), f32[8,1,1024]{2,1,0:T(1,128)S(1)}, u32[]{:S(2)}, u32[]{:S(2)}) async-start(f32[8,1,1024]{2,1,0:T(1,128)} %reshape.268), calls=%async_computation.2 | async-start | bytes 65536 | tf_op jit(solution)/shard_map/all_to_all | solution.py:28
  789.3 12.6 %all-to-all-start.3 = ((f32[8,1,3072]{2,1,0:T(1,128)}), f32[8,1,3072]{2,1,0:T(1,128)S(1)}, u32[]{:S(2)}, u32[]{:S(2)}) async-start(f32[8,1,3072]{2,1,0:T(1,128)} %reshape.270), calls=%async_computation.3 | async-start | bytes 196608 | tf_op jit(solution)/shard_map/all_to_all | solution.py:61
  (3 other events, 2.8 us)
Sparse Core Ops, SparseCore 0:
  43.7 92.1 all-gather.2
where the time goes:
time: 823 us; the launch traced here: 812 us
  local copies, waits for them, and re-layouts  430 us (52%)
  waiting for transfers between devices  118 us (14%)
  blocking collectives  91.2 us (11%)
  other arithmetic  56 us (7%)
  starting transfers between devices  50.6 us (6%)
  matrix products  41.6 us (5%)
  between operations  23.8 us (3%)
    unnamed x100, local copies, waits for them, and re-layouts  109 us
    all_gather x1, waiting for transfers between devices, total_of_pieces(): tiles = lax.all_gather(array, axis)  92.3 us
    psum x1, blocking collectives, shards(): lax.psum((buffer, grad_band, error_sum), ('enc', 'bin', 'off'))  91.2 us
    gather x2, local copies, waits for them, and re-layouts, count_cells(): inside = jnp.take(running, farthest) - jnp.take(running, places)  68.6 us
    reshape x1, local copies, waits for them, and re-layouts, diagonal_sums(): return jnp.sum(flat.reshape(chans, tile_rows, width - 1), axis=1)  43.9 us
    dynamic_slice x1, local copies, waits for them, and re-layouts, shards(): lax.dynamic_slice(framed_band, (0, LARGEST_DILATION + bin_displacement *...  37.5 us
    dynamic_slice x1, local copies, waits for them, and re-layouts, shards(): lax.dynamic_slice(framed_grad, (0, LARGEST_DILATION - bin_displacement *...  37.3 us
    reshape x1, local copies, waits for them, and re-layouts, hankel(): jnp.broadcast_to(base[:, None, :], (chans, tile_rows, width - 1))  21.4 us
  transfers between devices with their start and end apart: 15, of which 6 were waited for; matrix products, arithmetic and copies ran while one was open for 16% of the time, Pallas kernels for 0%

commit v1 on v0

v1 whole, which is shorter than its diff:
```python
import jax
import jax.numpy as jnp
from jax import lax
from jax.experimental import pallas as pl
from jax.experimental.pallas import tpu as pltpu
from jax.sharding import PartitionSpec as P

LARGEST_DILATION = 8
HALO = LARGEST_DILATION
EDGE = 2 * LARGEST_DILATION
F32 = jnp.float32
BF16 = jnp.bfloat16
MASKED = -1e38
GROUP = ("bin", "off")
EVERY = ("enc", "bin", "off")


def with_halo(cells, axis, dim, width):
    count = lax.axis_size(axis)
    ends = count - 1
    head = lax.slice_in_dim(cells, 0, width, axis=dim)
    tail = lax.slice_in_dim(cells, cells.shape[dim] - width, cells.shape[dim], axis=dim)
    return jnp.concatenate(
        [
            lax.ppermute(tail, axis, [(i, (i + 1) % count) for i in range(ends)]),
            cells,
            lax.ppermute(head, axis, [((i + 1) % count, i) for i in range(ends)]),
        ],
        axis=dim,
    )


def exchange(array, axis):
    return lax.all_to_all(array, axis, 0, 0, tiled=True)


def from_everyone(array, axis):
    return exchange(jnp.broadcast_to(array[None], (lax.axis_size(axis), *array.shape)), axis)


def pieces(x, shift):
    return [
        pltpu.roll(x[:, start : start + 128], shift, 1) for start in range(0, x.shape[1], 128)
    ]


def moved_right(x, shift):
    parts = pieces(x, shift)
    edge = lax.broadcasted_iota(jnp.int32, parts[0].shape, 1) < shift
    return jnp.concatenate(
        [jnp.where(edge, parts[k - 1], parts[k]) for k in range(len(parts))], axis=1
    )


def moved_left(x, shift):
    parts = pieces(x, 128 - shift)
    edge = lax.broadcasted_iota(jnp.int32, parts[0].shape, 1) < 128 - shift
    return jnp.concatenate(
        [jnp.where(edge, parts[k], parts[(k + 1) % len(parts)]) for k in range(len(parts))],
        axis=1,
    )


def count_body(flags_ref, flags_t_ref, limit_ref, out_ref):
    total = limit_ref.shape[1]
    chunk = 512
    flags_t = flags_t_ref[...].astype(BF16)
    high = flags_t.shape[1]
    place = lax.broadcasted_iota(jnp.int32, (128, 128), 0)
    other = lax.broadcasted_iota(jnp.int32, (128, 128), 1)
    before = jnp.where(other < place, 1.0, 0.0).astype(BF16)
    row_h = lax.broadcasted_iota(jnp.int32, (high, high), 0)
    col_h = lax.broadcasted_iota(jnp.int32, (high, high), 1)
    before_h = jnp.where(row_h < col_h, 1.0, 0.0).astype(BF16)
    inner = jnp.dot(before, flags_t, preferred_element_type=F32)
    outer = jnp.sum(jnp.dot(flags_t, before_h, preferred_element_type=F32), axis=0, keepdims=True)
    table = inner + outer
    table_hi = jnp.floor(table * (1.0 / 128.0))
    table_lo = (table - 128.0 * table_hi).astype(BF16)
    table_hi = table_hi.astype(BF16)
    row_of = lax.broadcasted_iota(jnp.int32, (high, chunk), 0)
    lane_of = lax.broadcasted_iota(jnp.int32, (128, chunk), 0)
    ids = lax.broadcasted_iota(jnp.int32, (1, chunk), 1)

    def looked_up(where):
        picks = jnp.where(row_of == lax.shift_right_logical(where, 7), 1.0, 0.0).astype(BF16)
        found = 128.0 * jnp.dot(table_hi, picks, preferred_element_type=F32) + jnp.dot(
            table_lo, picks, preferred_element_type=F32
        )
        return jnp.sum(
            jnp.where(lane_of == (where & 127), found, 0.0), axis=0, keepdims=True
        )

    acc = jnp.zeros((1, chunk), F32)
    for start in range(0, total, chunk):
        here = ids + start
        far = jnp.minimum(here + limit_ref[:, start : start + chunk], total)
        inside = looked_up(far) - looked_up(here)
        acc = acc + flags_ref[:, start : start + chunk].astype(F32) * inside
    out_ref[...] = jnp.broadcast_to(jnp.sum(acc, axis=1, keepdims=True), out_ref.shape)


def count_cells(valid_bins, offset_limit):
    total = valid_bins.shape[0]
    rows = -(-(total // 128 + 1) // 128) * 128
    flags = jnp.zeros((rows, 128), jnp.int32)
    flags = lax.dynamic_update_slice(flags, valid_bins.reshape(total // 128, 128), (0, 0))
    return pl.pallas_call(
        count_body, out_shape=jax.ShapeDtypeStruct((8, 128), F32), name="count"
    )(valid_bins[None], flags.astype(F32).T, offset_limit[None])


def band_body(
    info_ref,
    embed_ref,
    flag_near_ref,
    flag_far_ref,
    limit_ref,
    target_ref,
    fwd_ref,
    back_ref,
    head_ref,
    count_ref,
    pred_ref,
    near_out,
    far_out,
    grad_out,
    err_out,
    lines,
    parts,
    dress,
    owns,
    weights,
    goals,
):
    wide = limit_ref.shape[1]
    chans = near_out.shape[0]
    cols, rows = pred_ref.shape
    steps = cols + 2 * EDGE
    first_mid, last_mid = HALO, steps - HALO
    dilation = info_ref[0]
    offs_start = info_ref[1]
    row_start = info_ref[2]
    extent = info_ref[3]
    length = info_ref[4]
    wide_far = embed_ref.shape[1]
    turn = 448
    lane = lax.broadcasted_iota(jnp.int32, (1, wide), 1)
    bins = row_start + jnp.where(lane < turn, lane, lane - wide)
    near = jnp.where(
        (bins >= 0) & (bins < length), moved_left(moved_left(embed_ref[:chans].astype(F32), EDGE)[:, :wide], EDGE), MASKED
    )
    near_of = (
        moved_right(near, dilation).astype(BF16),
        near.astype(BF16),
        moved_left(near, dilation).astype(BF16),
    )
    flag_near = moved_left(jnp.broadcast_to(flag_near_ref[...], (8, wide)), EDGE)
    limit = moved_left(jnp.broadcast_to(limit_ref[...], (8, wide)), EDGE)
    goals[...] = moved_left(target_ref[...], EDGE)
    far = moved_left(embed_ref[chans:].astype(F32), HALO).astype(BF16)
    flags = moved_left(jnp.broadcast_to(flag_far_ref[...], (8, wide_far)), HALO)
    tiles = wide // 128
    tiles_far = wide_far // 128
    lane_tile = lax.broadcasted_iota(jnp.int32, (chans, 128), 1)
    before_turn = lane_tile < turn % 128

    def shifted(rolled, shift, extra, last_only):
        keep = last_only < 128 - shift

        def part(k):
            return jnp.where(keep, rolled[k % tiles_far], rolled[(k + 1) % tiles_far])

        out = [part(k + extra) for k in range(tiles)]
        out[-1] = jnp.where(last_only < turn % 128, out[-1], part(tiles + extra))
        return jnp.concatenate(out, axis=1)

    def make_line(shift, extra):
        turned = (128 - shift) & 127
        rolled = pieces(far, turned)
        rolled_flags = pieces(flags, turned)
        for more in range(extra):
            u = shift + 128 * more
            lines[u] = shifted(rolled, shift, more, lane_tile)
            flag = shifted(rolled_flags, shift, more, lane_tile[:8])
            offset = offs_start + u - HALO - EDGE
            offset = jnp.where(offset >= 0, offset, extent).astype(F32)
            weights[u] = jnp.where(limit > offset, flag_near * flag, 0.0)

    total_lines = steps + 2 * HALO
    both = total_lines - 128

    @pl.loop(0, both, unroll=8)
    def _(shift):
        make_line(shift, 2)

    @pl.loop(both, 128, unroll=8)
    def _(shift):
        make_line(shift, 1)

    def act_of(t, tap, width):
        line = lines[t + HALO + (tap - 1) * dilation, :, :width]
        return jnp.maximum(near_of[tap][:, :width] + line, jnp.zeros((), BF16))

    fwd = fwd_ref[...]

    @pl.loop(0, steps, unroll=40)
    def _(t):
        stacked = jnp.concatenate([act_of(t, tap, wide) for tap in range(3)], axis=0)
        parts[t] = jnp.dot(fwd, stacked, preferred_element_type=F32)

    @pl.when(offs_start == 0)
    def _():
        @pl.loop(0, EDGE)
        def _(t):
            parts[t] = jnp.zeros((3 * chans, wide), F32)

    @pl.when(offs_start + cols == extent)
    def _():
        @pl.loop(steps - EDGE, steps)
        def _(t):
            parts[t] = jnp.zeros((3 * chans, wide), F32)

    owns[:EDGE] = jnp.zeros((EDGE, chans, rows), BF16)
    owns[steps - EDGE :] = jnp.zeros((EDGE, chans, rows), BF16)
    head = jnp.broadcast_to(head_ref[...], (chans, wide))
    scale = 2.0 / (1.0 + count_ref[0:1, 0:1])

    def make_dres(t, err, own):
        conv = (
            parts[t - dilation, :chans]
            + parts[t, chans : 2 * chans]
            + parts[t + dilation, 2 * chans :]
        )
        resid = (near + lines[t + HALO].astype(F32)) + conv
        pred = jnp.sum(head * jnp.maximum(resid, 0.0), axis=0, keepdims=True)
        differ = pred - goals[pl.ds(t - HALO, 1)]
        weighted = weights[t + HALO, 0:1] * differ
        dres = jnp.where(resid > 0.0, head * (weighted * scale), 0.0).astype(BF16)
        dress[t] = dres
        if own:
            owns[t] = dres[:, :rows]
            pred_ref[pl.ds(t - EDGE, 1)] = pred[:, :rows]
            err = err + (weighted * differ)[:, :rows]
        return err

    err = jnp.zeros((1, rows), F32)
    err = lax.fori_loop(first_mid, EDGE, lambda t, e: make_dres(t, e, False), err, unroll=4)
    err = lax.fori_loop(EDGE, steps - EDGE, lambda t, e: make_dres(t, e, True), err, unroll=8)
    err = lax.fori_loop(
        steps - EDGE, last_mid, lambda t, e: make_dres(t, e, False), err, unroll=4
    )
    err_out[...] = jnp.broadcast_to(jnp.sum(err, axis=1, keepdims=True), err_out.shape)
    back = back_ref[...]

    @pl.loop(first_mid, last_mid, unroll=36)
    def _(t):
        dres = dress[t]
        stacked = jnp.concatenate(
            [
                moved_left(dres, dilation)[:, :rows],
                dres[:, :rows],
                moved_right(dres, dilation)[:, :rows],
            ],
            axis=0,
        )
        parts[t, :, :rows] = jnp.dot(back, stacked, preferred_element_type=F32)

    bunch = 8

    def make_grads(n, carry):
        near_sum, far_sum = carry
        far_sum = moved_right(far_sum, bunch)
        for k in range(bunch):
            t = steps - EDGE - bunch - n * bunch + k
            dact = (
                parts[t + dilation, :chans, :rows]
                + parts[t, chans : 2 * chans, :rows]
                + parts[t - dilation, 2 * chans :, :rows]
            )
            act = act_of(t, 1, rows).astype(F32)
            dpair = owns[t].astype(F32) + jnp.where(act > 0.0, dact, 0.0)
            near_sum = near_sum + dpair
            dpair = jnp.concatenate([dpair, jnp.zeros((chans, wide - rows), F32)], axis=1)
            far_sum = far_sum + (moved_right(dpair, k) if k else dpair)
        return near_sum, far_sum

    near_sum, far_sum = lax.fori_loop(
        0,
        cols // bunch,
        make_grads,
        (jnp.zeros((chans, rows), F32), jnp.zeros((chans, wide), F32)),
    )
    near_out[...] = near_sum
    far_out[...] = far_sum
    grad_out[...] = jnp.zeros((3 * chans, 3 * chans), F32)

    def add_weight_grads(first, batch):
        left = jnp.concatenate(
            [
                jnp.concatenate([act_of(first + k, tap, rows) for tap in range(3)], axis=0)
                for k in range(batch)
            ],
            axis=1,
        )
        right = jnp.concatenate(
            [
                jnp.concatenate([owns[first + k + move * dilation] for k in range(batch)], axis=1)
                for move in (1, 0, -1)
            ],
            axis=0,
        )
        grad_out[...] += lax.dot_general(
            left, right, (((1,), (1,)), ((), ())), preferred_element_type=F32
        )

    batch = 16

    @pl.loop(0, cols // batch)
    def _(n):
        add_weight_grads(EDGE + n * batch, batch)

    @pl.when(offs_start > 0)
    def _():
        add_weight_grads(first_mid, HALO)

    @pl.when(offs_start + cols < extent)
    def _():
        add_weight_grads(steps - EDGE, HALO)


def band(info, embed, flag_near, flag_far, limit, target, fwd, back, head, count, rows, cols):
    chans = embed.shape[0] // 2
    wide = limit.shape[1]
    steps = cols + 2 * EDGE
    vmem = pl.BlockSpec(memory_space=pltpu.VMEM)
    return pl.pallas_call(
        band_body,
        out_shape=(
            jax.ShapeDtypeStruct((cols, rows), F32),
            jax.ShapeDtypeStruct((chans, rows), F32),
            jax.ShapeDtypeStruct((chans, wide), F32),
            jax.ShapeDtypeStruct((3 * chans, 3 * chans), F32),
            jax.ShapeDtypeStruct((8, 128), F32),
        ),
        in_specs=[pl.BlockSpec(memory_space=pltpu.SMEM)] + [vmem] * 9,
        out_specs=(vmem,) * 5,
        scratch_shapes=[
            pltpu.VMEM((steps + 2 * HALO, chans, wide), BF16),
            pltpu.VMEM((steps, 3 * chans, wide), F32),
            pltpu.VMEM((steps, chans, wide), BF16),
            pltpu.VMEM((steps, chans, rows), BF16),
            pltpu.VMEM((steps + 2 * HALO, 8, wide), F32),
            pltpu.VMEM((steps - 2 * HALO, wide), F32),
        ],
        compiler_params=pltpu.CompilerParams(vmem_limit_bytes=60 * 1024 * 1024),
        name="band",
    )(info, embed, flag_near, flag_far, limit, target, fwd, back, head, count)


def place(info_ref, b, o, rows, cols):
    return pl.multiple_of(b * rows + info_ref[0] * (info_ref[1] + o * cols), 128)


def windows_body(n_off, rows, cols, info_ref, tiles_ref, out_ref, line):
    n_enc, each, bins = tiles_ref.shape
    lead = 2 * EDGE
    line[...] = jnp.zeros(line.shape, F32)
    whole = jnp.concatenate(
        [tiles_ref[e].astype(F32) for e in range(n_enc)] + [jnp.zeros((each, 128), F32)], axis=1
    )
    line[:, : n_enc * bins + 128] = moved_right(whole, lead)
    for index in range(out_ref.shape[0]):
        start = place(info_ref, index // n_off, index % n_off, rows, cols)
        out_ref[index] = line[:, pl.ds(start, out_ref.shape[2])].astype(out_ref.dtype)


def windows(info, tiles, n_bin, n_off, rows, cols, wide):
    n_enc, each, bins = tiles.shape
    return pl.pallas_call(
        lambda *refs: windows_body(n_off, rows, cols, *refs),
        out_shape=jax.ShapeDtypeStruct((n_bin * n_off, each, wide), tiles.dtype),
        in_specs=[
            pl.BlockSpec(memory_space=pltpu.SMEM),
            pl.BlockSpec(memory_space=pltpu.VMEM),
        ],
        out_specs=pl.BlockSpec(memory_space=pltpu.VMEM),
        scratch_shapes=[
            pltpu.VMEM((each, (n_bin - 1) * rows + n_enc * n_off * cols + wide + 128), F32)
        ],
        name="windows",
    )(info, tiles)


def lines_body(n_off, rows, cols, wide, info_ref, parts_ref, out_ref, line):
    n_enc, each, total = out_ref.shape
    bins = total - (parts_ref.shape[2] - wide)
    line[...] = jnp.zeros(line.shape, F32)
    extra = parts_ref[0, :, wide:]
    for index in range(parts_ref.shape[0]):
        start = place(info_ref, index // n_off, index % n_off, rows, cols)
        line[:, pl.ds(start, wide)] += parts_ref[index, :, :wide]
        if index:
            extra = extra + parts_ref[index, :, wide:]
    for e in range(n_enc):
        out_ref[e, :, :bins] = line[:, e * bins : (e + 1) * bins]
        out_ref[e, :, bins:] = extra


def lines_of(info, parts, n_enc, n_off, bins, rows, cols, wide):
    group, each, total = parts.shape
    return pl.pallas_call(
        lambda *refs: lines_body(n_off, rows, cols, wide, *refs),
        out_shape=jax.ShapeDtypeStruct((n_enc, each, bins + total - wide), F32),
        in_specs=[
            pl.BlockSpec(memory_space=pltpu.SMEM),
            pl.BlockSpec(memory_space=pltpu.VMEM),
        ],
        out_specs=pl.BlockSpec(memory_space=pltpu.VMEM),
        scratch_shapes=[
            pltpu.VMEM((each, group // n_off * rows + n_enc * n_off * cols + wide), F32)
        ],
        name="lines",
    )(info, parts)


def shards(
    encoder_in,
    gain_enc,
    conv_one,
    proj_weight,
    conv_two,
    head_weight,
    target,
    valid_bins,
    offset_limit,
    dilations,
):
    chans, encoder_bins = encoder_in.shape
    width_in = conv_one.shape[2]
    second = conv_two.shape[1]
    rows, cols = target.shape
    n_enc, n_bin, n_off = (lax.axis_size(axis) for axis in EVERY)
    group = n_bin * n_off
    each = 2 * second // group
    length = valid_bins.shape[0]
    extent = cols * n_enc * n_off
    first_dilation = dilations[0]
    second_dilation = dilations[1]
    enc_id, bin_id, off_id = (lax.axis_index(axis) for axis in EVERY)
    row_start = bin_id * rows
    tile_id = enc_id * n_off + off_id
    offs_start = tile_id * cols

    activ = jax.nn.gelu(gain_enc[:, None] * encoder_in.astype(F32)).astype(BF16)
    framed = with_halo(activ, "enc", 1, HALO)
    framed_bins = encoder_bins + 2 * HALO
    everywhere = from_everyone(framed, GROUP).reshape(width_in, framed_bins)
    count = count_cells(valid_bins, offset_limit)
    goal = with_halo(target.T, "bin", 1, HALO)
    goal = with_halo(goal, ("enc", "off"), 0, HALO)

    weight_one = conv_one.reshape(3 * chans, width_in)
    taps = jnp.dot(weight_one, everywhere, preferred_element_type=F32)
    conv_out = sum(
        lax.dynamic_slice(
            taps, (tap * chans, HALO + (tap - 1) * first_dilation), (chans, encoder_bins)
        )
        for tap in range(3)
    )
    hidden = (encoder_in.astype(F32) + conv_out).astype(BF16)
    proj_rows = jnp.transpose(proj_weight, (0, 2, 1)).reshape(2 * second, chans)
    partial_embed = jnp.dot(proj_rows, hidden, preferred_element_type=F32)
    summed = exchange(partial_embed.reshape(group, each, encoder_bins), GROUP).sum(axis=0)
    tiles = from_everyone(summed.astype(BF16), "enc")
    wide = 512
    wide_far = 640
    is_far = (bin_id * n_off + off_id) * each >= second
    spots = jnp.stack([is_far.astype(jnp.int32), enc_id * n_off * cols]).astype(jnp.int32)
    embed = exchange(windows(spots, tiles, n_bin, n_off, rows, cols, wide_far), GROUP)
    embed = embed.reshape(2 * second, wide_far)
    flags = jnp.pad(valid_bins.astype(F32), (2 * EDGE, extent + wide_far))[None]
    flag_near = lax.dynamic_slice_in_dim(flags, row_start + EDGE, wide, 1)
    flag_far = lax.dynamic_slice_in_dim(flags, row_start + offs_start, wide_far, 1)
    limits = jnp.pad(offset_limit.astype(F32), (EDGE, wide))[None]
    limit = lax.dynamic_slice_in_dim(limits, row_start, wide, 1)
    goal = jnp.pad(goal.astype(F32), ((0, 0), (HALO, wide - rows - 3 * HALO)))
    info = jnp.stack(
        [second_dilation, offs_start, row_start, jnp.int32(extent), jnp.int32(length)]
    ).astype(jnp.int32)
    taps_two = conv_two.reshape(3, 3, second, second)
    fwd = jnp.transpose(taps_two, (1, 3, 0, 2)).reshape(3 * second, 3 * second)
    back = jnp.transpose(taps_two, (1, 2, 0, 3)).reshape(3 * second, 3 * second)
    pred, near_grad, far_grad, band_grad, error = band(
        info,
        embed,
        flag_near,
        flag_far,
        limit,
        goal,
        fwd,
        back,
        head_weight[:, None],
        count,
        rows,
        cols,
    )
    prediction = pred.T

    size = 9 * second * second
    share = size // group
    pad_share = -(-(share + 1) // (each * 128)) * 128
    extra = jnp.concatenate(
        [band_grad.reshape(group, share), jnp.broadcast_to(error[0:1, 0:1], (group, 1))], axis=1
    )
    extra = jnp.pad(extra, ((0, 0), (0, each * pad_share - share - 1)))
    parts = jnp.concatenate(
        [jnp.pad(near_grad, ((0, 0), (0, wide - rows))), far_grad], axis=0
    ).reshape(group, each, wide)
    parts = jnp.concatenate([parts, extra.reshape(group, each, pad_share)], axis=2)
    parts = lines_of(
        spots, exchange(parts, GROUP), n_enc, n_off, encoder_bins, rows, cols, wide
    )
    parts = exchange(parts, "enc").sum(axis=0)
    grad_embed = parts[:, :encoder_bins].astype(BF16).astype(F32)
    gathered = from_everyone(
        jnp.concatenate([grad_embed, parts[:, encoder_bins:]], axis=1), GROUP
    )
    grad_rows = gathered[:, :, :encoder_bins].reshape(2 * second, encoder_bins).astype(BF16)
    extra = gathered[:, :, encoder_bins:].reshape(group, each * pad_share)
    grad_conv_two = (
        extra[:, :share]
        .reshape(3, second, 3, second)
        .transpose(0, 2, 1, 3)
        .reshape(9, second, second)
    )
    loss_mean = extra[0, share : share + 1] / (1.0 + count[0, 0:1])

    dhidden = jnp.dot(proj_rows.T, grad_rows, preferred_element_type=F32).astype(BF16)
    proj_local = lax.dot_general(
        hidden, grad_rows, (((1,), (1,)), ((), ())), preferred_element_type=F32
    )
    proj_local = jnp.transpose(proj_local.reshape(chans, 2, second), (1, 0, 2))
    shifted = jnp.concatenate(
        [
            lax.dynamic_update_slice(
                jnp.zeros((chans, framed_bins), BF16),
                dhidden,
                (0, HALO + (tap - 1) * first_dilation),
            )
            for tap in range(3)
        ],
        axis=0,
    )
    conv_local = lax.dot_general(
        shifted, everywhere, (((1,), (1,)), ((), ())), preferred_element_type=F32
    )
    own_width = width_in // n_enc
    conv_size = 3 * chans * own_width
    proj_size = 2 * chans * second
    conv_local = jnp.transpose(
        conv_local.reshape(3 * chans, n_enc, own_width), (1, 0, 2)
    ).reshape(n_enc, conv_size // 128, 128)
    common = proj_local.reshape(proj_size // 128, 128)
    final = exchange(
        jnp.concatenate(
            [conv_local, jnp.broadcast_to(common[None], (n_enc, *common.shape))], axis=1
        ),
        "enc",
    ).sum(axis=0)
    grad_conv_one = final[: conv_size // 128].reshape(3, chans, own_width)
    grad_proj = final[conv_size // 128 :].reshape(2, chans, second)
    return (prediction, loss_mean, grad_conv_two, grad_proj, grad_conv_one)


def solution(mesh):
    in_specs = (
        P(("bin", "off"), "enc"),
        P(("bin", "off")),
        P(None, ("bin", "off"), None),
        P(None, ("bin", "off"), None),
        P(),
        P(),
        P("bin", ("enc", "off")),
        P(),
        P(),
        P(),
    )
    out_specs = (
        P("bin", ("enc", "off")),
        P(),
        P(),
        P(None, ("bin", "off"), None),
        P(None, ("bin", "off"), "enc"),
    )
    return jax.shard_map(shards, mesh=mesh, in_specs=in_specs, out_specs=out_specs, check_vma=False)
```

time: 823 us -> 177 us (0.22); the launches traced: 812 us -> 176 us
  local copies, waits for them, and re-layouts: 430 us -> 22.3 us
  waiting for transfers between devices: 118 us -> 17.1 us
  other arithmetic: 56 us -> 4.69 us
  blocking collectives: 91.2 us -> 40.8 us
  matrix products: 41.6 us -> 1.41 us
  Pallas kernels: 0 us -> 34.4 us
  between operations: 23.8 us -> 5.48 us
    unnamed x100 -> x29, local copies, waits for them, and re-layouts: 109 us -> 5.5 us
    all_gather x1 -> x0, waiting for transfers between devices: 92.3 us -> none  [total_of_pieces(): tiles = lax.all_gather(array, axis)]
    psum x1 -> x0, blocking collectives: 91.2 us -> none  [shards(): lax.psum((buffer, grad_band, error_sum), ('enc', 'bin', 'off'))]
    dynamic_slice x6 -> x1, local copies, waits for them, and re-layouts: 77.5 us -> 0.59 us  [shards(): lax.dynamic_slice_in_dim(flags, row_start + offs_start, wide_far, 1)]
    gather x2 -> x0, local copies, waits for them, and re-layouts: 68.6 us -> none  [count_cells(): inside = jnp.take(running, farthest) - jnp.take(running, places)]
    reshape x8 -> x15, local copies, waits for them, and re-layouts: 71.7 us -> 5.78 us  [the longest x1 0.87 us: shards(): band_grad.reshape(group, share)]
    all_to_all x0 -> x3, blocking collectives: none -> 40.8 us  [exchange(): return lax.all_to_all(array, axis, 0, 0, tiled=True)]
    dot_general x7 -> x5, matrix products: 41.6 us -> 1.41 us  [the longest x1 0.59 us: shards(): lax.dot_general(shifted, everywhere, (((1,), (1,)), ((), ())), preferred_...]
  transfers between devices with their start and end apart: 15 -> 11, of which waited for: 6 -> 5; matrix products, arithmetic and copies ran while one was open for 16% -> 8% of each run, Pallas kernels for 0% -> 3%
where the time goes in v1:
time: 177 us; the launch traced here: 176 us
  starting transfers between devices  49.7 us (28%)
  blocking collectives  40.8 us (23%)
  Pallas kernels  34.4 us (19%)
  local copies, waits for them, and re-layouts  22.3 us (13%)
  waiting for transfers between devices  17.1 us (10%)
  between operations  5.48 us (3%)
  other arithmetic  4.69 us (3%)
    all_to_all x3, blocking collectives, exchange(): return lax.all_to_all(array, axis, 0, 0, tiled=True)  40.8 us
    all_to_all x5, starting transfers between devices, exchange(): return lax.all_to_all(array, axis, 0, 0, tiled=True)  33.7 us
    pallas_call x1, Pallas kernels, band(): pl.pallas_call(band_body, out_shape=(jax.ShapeDtypeStruct((cols, rows), F...  26.6 us
    all_to_all x5, waiting for transfers between devices, exchange(): return lax.all_to_all(array, axis, 0, 0, tiled=True)  15.8 us
    ppermute x3, starting transfers between devices, with_halo(): lax.ppermute(tail, axis, [(i, (i + 1) % count) for i in range(ends)])  11.4 us
    unnamed x29, local copies, waits for them, and re-layouts  5.5 us
    ppermute x3, starting transfers between devices, with_halo(): lax.ppermute(head, axis, [((i + 1) % count, i) for i in range(ends)])  4.58 us
    pallas_call x1, Pallas kernels, count_cells(): pl.pallas_call(count_body, out_shape=jax.ShapeDtypeStruct((8, 128), F32),...  4.36 us
  transfers between devices with their start and end apart: 11, of which 5 were waited for; matrix products, arithmetic and copies ran while one was open for 8% of the time, Pallas kernels for 3%

profile of v1, /device:TPU:2, one launch (start us, length us, event | category | flops | bytes accessed | tf_op | source)
XLA Modules:
  0.0 175.8 jit_solution(7733408748760962710)
XLA Ops:
  0.6 0.8 fusion.21
  1.6 1.3 collective-permute-start.1
  2.9 4.5 %collective-permute-start = (bf16[16,8]{1,0:T(8,128)(2,1)S(1)}, bf16[16,8]{1,0:T(8,128)(2,1)S(1)}, u32[]{:S(2)}, u32[]{:S(2)}) collective-permute-start(bf16[16,8]{1,0:T(8,128)(2,1)S(1)} %get-tuple-element.34), channel_id=1, source_target_pairs={{0,32},{32,64},{64,96},{96,128},{128,160},{160,192},{192,224},{1,3... | collective-permute-start | bytes 776 | tf_op jit(solution)/shard_map/ppermute | solution.py:25
  7.4 1.3 collective-permute-done
  8.8 1.0 broadcast_in_dim.18
  9.8 7.8 %all-to-all-start = ((bf16[32,16,784]{2,1,0:T(8,128)(2,1)}), bf16[32,16,784]{2,1,0:T(8,128)(2,1)S(1)}, u32[]{:S(2)}, u32[]{:S(2)}) async-start(bf16[32,16,784]{2,1,0:T(8,128)(2,1)} %broadcast_in_dim.18), calls=%async_computation | async-start | bytes 1835008 | tf_op jit(solution)/shard_map/all_to_all | solution.py:34
  17.8 2.0 %collective-permute-start.3 = (bf16[128,8]{1,0:T(8,128)(2,1)S(1)}, bf16[128,8]{1,0:T(8,128)(2,1)S(1)}, u32[]{:S(2)}, u32[]{:S(2)}) collective-permute-start(bf16[128,8]{1,0:T(8,128)(2,1)S(1)} %get-tuple-element.33), channel_id=1, source_target_pairs={{2,0},{4,2},{6,4},{8,6},{10,8},{12,10},{14,12},{16,14},{18,16},{20... | collective-permute-start | bytes 6152 | tf_op jit(solution)/shard_map/ppermute | solution.py:27
  19.8 2.3 %collective-permute-start.2 = (bf16[128,8]{1,0:T(8,128)(2,1)S(1)}, bf16[128,8]{1,0:T(8,128)(2,1)S(1)}, u32[]{:S(2)}, u32[]{:S(2)}) collective-permute-start(bf16[128,8]{1,0:T(8,128)(2,1)S(1)} %get-tuple-element.32), channel_id=1, source_target_pairs={{0,2},{2,4},{4,6},{6,8},{8,10},{10,12},{12,14},{14,16},{16,18},{18... | collective-permute-start | bytes 6152 | tf_op jit(solution)/shard_map/ppermute | solution.py:25
  22.2 0.6 copy-done.11
  25.4 0.7 copy-done.10
  26.2 0.7 copy-done.6
  27.0 0.7 pad_dynamic-slice_fusion.1
  28.4 4.7 %all-to-all-done = bf16[32,16,784]{2,1,0:T(8,128)(2,1)S(1)} async-done(((bf16[32,16,784]{2,1,0:T(8,128)(2,1)}), bf16[32,16,784]{2,1,0:T(8,128)(2,1)S(1)}, u32[]{:S(2)}, u32[]{:S(2)}) %all-to-all-start) | async-done | bytes 802848 | tf_op jit(solution)/shard_map/all_to_all | solution.py:34
  34.1 0.8 reshape.101
  34.9 5.5 %all-to-all-start.1 = ((f32[32,2,768]{2,1,0:T(2,128)}), f32[32,2,768]{2,1,0:T(2,128)S(1)}, u32[]{:S(2)}, u32[]{:S(2)}) async-start(f32[32,2,768]{2,1,0:T(2,128)} %reshape.101), calls=%async_computation.1 | async-start | bytes 393216 | tf_op jit(solution)/shard_map/all_to_all | solution.py:34
  40.4 0.7 pad_dynamic-slice_fusion.2
  41.1 1.3 collective-permute-start.5
  42.4 4.5 %collective-permute-start.4 = (bf16[8,400]{1,0:T(8,128)(2,1)S(1)}, bf16[8,400]{1,0:T(8,128)(2,1)S(1)}, u32[]{:S(2)}, u32[]{:S(2)}) collective-permute-start(bf16[8,400]{1,0:T(8,128)(2,1)S(1)} %get-tuple-element.30), channel_id=1, source_target_pairs={{0,1},{1,32},{32,33},{33,64},{64,65},{65,96},{96,97},{97,128},{128... | collective-permute-start | bytes 19208 | tf_op jit(solution)/shard_map/ppermute | solution.py:25
  47.0 1.1 all-to-all-done.1
  48.8 10.0 %all-to-all-start.2 = ((bf16[8,2,768]{2,1,0:T(2,128)(2,1)}), bf16[8,2,768]{2,1,0:T(2,128)(2,1)S(1)}, u32[]{:S(2)}, u32[]{:S(2)}) async-start(bf16[8,2,768]{2,1,0:T(2,128)(2,1)} %broadcast_in_dim.19), calls=%async_computation.2 | async-start | bytes 49152 | tf_op jit(solution)/shard_map/all_to_all | solution.py:34
  60.2 0.7 reshape.104.fwd_ref
  60.9 0.7 reshape.105.back_ref
  61.6 0.7 copy-done.12
  62.3 0.7 copy.33.head_ref
  63.0 4.4 %count.1.count_ref = f32[8,128]{1,0:T(8,128)} custom-call(s32[1,6144]{1,0:T(1,128)} %bitcast.75, f32[128,128]{1,0:T(8,128)} %convert_bitcast_fusion.flags_t_ref, s32[1,6144]{1,0:T(1,128)} %bitcast.81), custom_call_target="tpu_custom_call" | custom-call | tf_op jit(solution)/shard_map/count/pallas_call | solution.py:108
  67.3 1.2 stack.23.info_ref
  69.1 1.6 windows.1
  70.7 6.9 %all-to-all-start.3 = ((bf16[32,2,640]{2,1,0:T(2,128)(2,1)}), bf16[32,2,640]{2,1,0:T(2,128)(2,1)S(1)}, u32[]{:S(2)}, u32[]{:S(2)}) async-start(bf16[32,2,640]{2,1,0:T(2,128)(2,1)} %windows.1), calls=%async_computation.3 | async-start | bytes 163840 | tf_op jit(solution)/shard_map/all_to_all | solution.py:34
  77.6 0.8 fusion.4.target_ref
  78.5 5.7 %all-to-all-done.3 = bf16[32,2,640]{2,1,0:T(2,128)(2,1)S(1)} async-done(((bf16[32,2,640]{2,1,0:T(2,128)(2,1)}), bf16[32,2,640]{2,1,0:T(2,128)(2,1)S(1)}, u32[]{:S(2)}, u32[]{:S(2)}) %all-to-all-start.3) | async-done | bytes 81952 | tf_op jit(solution)/shard_map/all_to_all | solution.py:34
  84.2 0.7 reshape.102.embed_ref
  84.9 26.6 %band.1 = (f32[128,384]{1,0:T(8,128)}, f32[32,384]{1,0:T(8,128)}, f32[32,512]{1,0:T(8,128)}, f32[96,96]{1,0:T(8,128)}, f32[8,128]{1,0:T(8,128)}) custom-call(s32[5]{0:T(128)} %stack.23.info_ref, bf16[64,640]{1,0:T(8,128)(2,1)} %reshape.102.embed_ref, f32[1,512]{1,0:T(1,128)} %bitcast.82, f32[1,640]{1,0:T(1,128)} %dynamic_slice.22.flag_far_ref, ...), custom_call_target="tpu_custom_call" | custom-call | tf_op jit(solution)/shard_map/band/pallas_call | solution.py:337
  111.5 0.9 reshape.108
  112.4 1.2 slice.63
  113.6 0.7 pad_select_fusion
  114.3 0.8 copy-done.8
  115.3 12.6 %all_to_all.40.refs_1_ = f32[32,2,768]{2,1,0:T(2,128)} all-to-all(f32[32,2,768]{2,1,0:T(2,128)S(1)} %pad_maximum_fusion), channel_id=1, replica_groups=mesh['enc'=8,'bin'=16,'off'=2] {'bin','off'}, dimensions={0} | all-to-all | bytes 393216 | tf_op jit(solution)/shard_map/all_to_all | solution.py:34
  127.9 1.8 %lines.1 = f32[8,2,1024]{2,1,0:T(2,128)} custom-call(s32[2]{0:T(128)} %pad_add_fusion.refs_0_, f32[32,2,768]{2,1,0:T(2,128)} %all_to_all.40.refs_1_), custom_call_target="tpu_custom_call" | custom-call | tf_op jit(solution)/shard_map/lines/pallas_call | solution.py:412
  129.6 15.7 %all_to_all.41 = f32[8,2,1024]{2,1,0:T(2,128)S(1)} all-to-all(f32[8,2,1024]{2,1,0:T(2,128)} %lines.1), channel_id=1, replica_groups=mesh['enc'=8,'bin'=16,'off'=2] {'enc'}, dimensions={0} | all-to-all | bytes 131072 | tf_op jit(solution)/shard_map/all_to_all | solution.py:34
  145.5 12.5 %all_to_all.42 = f32[32,2,1024]{2,1,0:T(2,128)S(1)} all-to-all(f32[32,2,1024]{2,1,0:T(2,128)S(1)} %broadcast_in_dim.24), channel_id=1, replica_groups=mesh['enc'=8,'bin'=16,'off'=2] {'bin','off'}, dimensions={0} | all-to-all | bytes 524288 | tf_op jit(solution)/shard_map/all_to_all | solution.py:34
  160.1 0.7 pad_maximum_fusion.1
  160.8 3.5 %all-to-all-start.7 = ((f32[8,32,128]{2,1,0:T(8,128)}), f32[8,32,128]{2,1,0:T(8,128)S(1)}, u32[]{:S(2)}, u32[]{:S(2)}) async-start(f32[8,32,128]{2,1,0:T(8,128)} %pad_maximum_fusion.1), calls=%async_computation.7 | async-start | bytes 262144 | tf_op jit(solution)/shard_map/all_to_all | solution.py:34
  164.3 1.2 slice.68
  166.1 0.8 copy.35
  167.7 0.7 copy.34
  169.0 4.3 %all-to-all-done.7 = f32[8,32,128]{2,1,0:T(8,128)S(1)} async-done(((f32[8,32,128]{2,1,0:T(8,128)}), f32[8,32,128]{2,1,0:T(8,128)S(1)}, u32[]{:S(2)}, u32[]{:S(2)}) %all-to-all-start.7) | async-done | bytes 131104 | tf_op jit(solution)/shard_map/all_to_all | solution.py:34
  173.3 0.7 reshape.114
  174.0 0.7 reshape.115
  (79 shorter events, 8.8 us)
Async XLA Ops:
  0.6 32.4 %copy-start = (bf16[3,16,512]{2,1,0:T(8,128)(2,1)S(1)}, bf16[3,16,512]{2,1,0:T(8,128)(2,1)}, u32[]{:S(2)}) copy-start(bf16[3,16,512]{2,1,0:T(8,128)(2,1)} %param.12) | copy-start | bytes 147460
  1.6 5.8 %collective-permute-start.1 = (bf16[16,8]{1,0:T(8,128)(2,1)S(1)}, bf16[16,8]{1,0:T(8,128)(2,1)S(1)}, u32[]{:S(2)}, u32[]{:S(2)}) collective-permute-start(bf16[16,8]{1,0:T(8,128)(2,1)S(1)} %get-tuple-element.35), channel_id=1, source_target_pairs={{32,0},{64,32},{96,64},{128,96},{160,128},{192,160},{224,192},{33,... | collective-permute-start | bytes 776 | tf_op jit(solution)/shard_map/ppermute | solution.py:27
  2.9 5.9 %collective-permute-start = (bf16[16,8]{1,0:T(8,128)(2,1)S(1)}, bf16[16,8]{1,0:T(8,128)(2,1)S(1)}, u32[]{:S(2)}, u32[]{:S(2)}) collective-permute-start(bf16[16,8]{1,0:T(8,128)(2,1)S(1)} %get-tuple-element.34), channel_id=1, source_target_pairs={{0,32},{32,64},{64,96},{96,128},{128,160},{160,192},{192,224},{1,3... | collective-permute-start | bytes 776 | tf_op jit(solution)/shard_map/ppermute | solution.py:25
  9.8 7.8 %copy-start.4 = (bf16[384,128]{1,0:T(8,128)(2,1)S(1)}, bf16[384,128]{1,0:T(8,128)(2,1)}, u32[]{:S(2)}) copy-start(bf16[384,128]{1,0:T(8,128)(2,1)} %param.16) | copy-start | bytes 294916
  9.8 23.2 %all-to-all-start = ((bf16[32,16,784]{2,1,0:T(8,128)(2,1)}), bf16[32,16,784]{2,1,0:T(8,128)(2,1)S(1)}, u32[]{:S(2)}, u32[]{:S(2)}) async-start(bf16[32,16,784]{2,1,0:T(8,128)(2,1)} %broadcast_in_dim.18), calls=%async_computation | async-start | bytes 1835008 | tf_op jit(solution)/shard_map/all_to_all | solution.py:34
  17.8 23.3 %collective-permute-start.3 = (bf16[128,8]{1,0:T(8,128)(2,1)S(1)}, bf16[128,8]{1,0:T(8,128)(2,1)S(1)}, u32[]{:S(2)}, u32[]{:S(2)}) collective-permute-start(bf16[128,8]{1,0:T(8,128)(2,1)S(1)} %get-tuple-element.33), channel_id=1, source_target_pairs={{2,0},{4,2},{6,4},{8,6},{10,8},{12,10},{14,12},{16,14},{18,16},{20... | collective-permute-start | bytes 6152 | tf_op jit(solution)/shard_map/ppermute | solution.py:27
  19.8 21.2 %collective-permute-start.2 = (bf16[128,8]{1,0:T(8,128)(2,1)S(1)}, bf16[128,8]{1,0:T(8,128)(2,1)S(1)}, u32[]{:S(2)}, u32[]{:S(2)}) collective-permute-start(bf16[128,8]{1,0:T(8,128)(2,1)S(1)} %get-tuple-element.32), channel_id=1, source_target_pairs={{0,2},{2,4},{4,6},{6,8},{8,10},{10,12},{12,14},{14,16},{16,18},{18... | collective-permute-start | bytes 6152 | tf_op jit(solution)/shard_map/ppermute | solution.py:25
  22.1 0.7 copy-start.11
  25.3 0.7 copy-start.10
  25.4 0.8 copy-start.2
  26.1 0.7 copy-start.6
  33.0 0.7 copy-start.5
  34.9 13.2 %all-to-all-start.1 = ((f32[32,2,768]{2,1,0:T(2,128)}), f32[32,2,768]{2,1,0:T(2,128)S(1)}, u32[]{:S(2)}, u32[]{:S(2)}) async-start(f32[32,2,768]{2,1,0:T(2,128)} %reshape.101), calls=%async_computation.1 | async-start | bytes 393216 | tf_op jit(solution)/shard_map/all_to_all | solution.py:34
  41.1 36.5 %collective-permute-start.5 = (bf16[8,400]{1,0:T(8,128)(2,1)S(1)}, bf16[8,400]{1,0:T(8,128)(2,1)S(1)}, u32[]{:S(2)}, u32[]{:S(2)}) collective-permute-start(bf16[8,400]{1,0:T(8,128)(2,1)S(1)} %get-tuple-element.31), channel_id=1, source_target_pairs={{1,0},{32,1},{33,32},{64,33},{65,64},{96,65},{97,96},{128,97},{129... | collective-permute-start | bytes 19208 | tf_op jit(solution)/shard_map/ppermute | solution.py:27
  42.4 35.2 %collective-permute-start.4 = (bf16[8,400]{1,0:T(8,128)(2,1)S(1)}, bf16[8,400]{1,0:T(8,128)(2,1)S(1)}, u32[]{:S(2)}, u32[]{:S(2)}) collective-permute-start(bf16[8,400]{1,0:T(8,128)(2,1)S(1)} %get-tuple-element.30), channel_id=1, source_target_pairs={{0,1},{1,32},{32,33},{33,64},{64,65},{65,96},{96,97},{97,128},{128... | collective-permute-start | bytes 19208 | tf_op jit(solution)/shard_map/ppermute | solution.py:25
  48.2 11.2 %copy-start.1 = (bf16[9,32,32]{2,1,0:T(8,128)(2,1)S(1)}, bf16[9,32,32]{2,1,0:T(8,128)(2,1)}, u32[]{:S(2)}) copy-start(bf16[9,32,32]{2,1,0:T(8,128)(2,1)} %param.14) | copy-start | bytes 55300
  48.8 19.7 %all-to-all-start.2 = ((bf16[8,2,768]{2,1,0:T(2,128)(2,1)}), bf16[8,2,768]{2,1,0:T(2,128)(2,1)S(1)}, u32[]{:S(2)}, u32[]{:S(2)}) async-start(bf16[8,2,768]{2,1,0:T(2,128)(2,1)} %broadcast_in_dim.19), calls=%async_computation.2 | async-start | bytes 49152 | tf_op jit(solution)/shard_map/all_to_all | solution.py:34
  61.6 0.7 copy-start.12
  68.5 0.6 copy-start.7
  70.7 13.5 %all-to-all-start.3 = ((bf16[32,2,640]{2,1,0:T(2,128)(2,1)}), bf16[32,2,640]{2,1,0:T(2,128)(2,1)S(1)}, u32[]{:S(2)}, u32[]{:S(2)}) async-start(bf16[32,2,640]{2,1,0:T(2,128)(2,1)} %windows.1), calls=%async_computation.3 | async-start | bytes 163840 | tf_op jit(solution)/shard_map/all_to_all | solution.py:34
  114.3 0.8 copy-start.8
  114.3 0.8 copy-start.9
  160.8 5.4 %copy-start.3 = (f32[128,384]{1,0:T(8,128)S(1)}, f32[128,384]{1,0:T(8,128)}, u32[]{:S(2)}) copy-start(f32[128,384]{1,0:T(8,128)} %get-tuple-element.10) | copy-start | bytes 589828
  160.8 12.5 %all-to-all-start.7 = ((f32[8,32,128]{2,1,0:T(8,128)}), f32[8,32,128]{2,1,0:T(8,128)S(1)}, u32[]{:S(2)}, u32[]{:S(2)}) async-start(f32[8,32,128]{2,1,0:T(8,128)} %pad_maximum_fusion.1), calls=%async_computation.7 | async-start | bytes 262144 | tf_op jit(solution)/shard_map/all_to_all | solution.py:34

commit v2 on v1

--- a/solution.py
+++ b/solution.py
@@ -61,60 +61,67 @@
     )
 
 
-def count_body(flags_ref, flags_t_ref, limit_ref, out_ref):
+def prep_body(flags_ref, square_ref, limit_ref, count_ref, flag_line, limit_line):
     total = limit_ref.shape[1]
-    chunk = 512
-    flags_t = flags_t_ref[...].astype(BF16)
-    high = flags_t.shape[1]
+    used = square_ref.shape[0]
+    high = -(-(used + 1) // 16) * 16
+    square = jnp.concatenate(
+        [square_ref[...].astype(F32), jnp.zeros((high - used, 128), F32)], axis=0
+    ).astype(BF16)
     place = lax.broadcasted_iota(jnp.int32, (128, 128), 0)
     other = lax.broadcasted_iota(jnp.int32, (128, 128), 1)
-    before = jnp.where(other < place, 1.0, 0.0).astype(BF16)
     row_h = lax.broadcasted_iota(jnp.int32, (high, high), 0)
     col_h = lax.broadcasted_iota(jnp.int32, (high, high), 1)
-    before_h = jnp.where(row_h < col_h, 1.0, 0.0).astype(BF16)
-    inner = jnp.dot(before, flags_t, preferred_element_type=F32)
-    outer = jnp.sum(jnp.dot(flags_t, before_h, preferred_element_type=F32), axis=0, keepdims=True)
-    table = inner + outer
+    inner = jnp.dot(
+        square, jnp.where(place < other, 1.0, 0.0).astype(BF16), preferred_element_type=F32
+    )
+    outer = jnp.dot(
+        jnp.where(col_h < row_h, 1.0, 0.0).astype(BF16), square, preferred_element_type=F32
+    )
+    table = inner + jnp.sum(outer, axis=1, keepdims=True)
     table_hi = jnp.floor(table * (1.0 / 128.0))
-    table_lo = (table - 128.0 * table_hi).astype(BF16)
-    table_hi = table_hi.astype(BF16)
+    tables = jnp.concatenate([table_hi, table - 128.0 * table_hi], axis=1).astype(BF16)
+    chunk = 512
     row_of = lax.broadcasted_iota(jnp.int32, (high, chunk), 0)
     lane_of = lax.broadcasted_iota(jnp.int32, (128, chunk), 0)
     ids = lax.broadcasted_iota(jnp.int32, (1, chunk), 1)
-
-    def looked_up(where):
-        picks = jnp.where(row_of == lax.shift_right_logical(where, 7), 1.0, 0.0).astype(BF16)
-        found = 128.0 * jnp.dot(table_hi, picks, preferred_element_type=F32) + jnp.dot(
-            table_lo, picks, preferred_element_type=F32
-        )
-        return jnp.sum(
-            jnp.where(lane_of == (where & 127), found, 0.0), axis=0, keepdims=True
-        )
-
     acc = jnp.zeros((1, chunk), F32)
     for start in range(0, total, chunk):
-        here = ids + start
-        far = jnp.minimum(here + limit_ref[:, start : start + chunk], total)
-        inside = looked_up(far) - looked_up(here)
+        far = jnp.minimum(ids + start + limit_ref[:, start : start + chunk], total)
+        picks = jnp.where(row_of == lax.shift_right_logical(far, 7), 1.0, 0.0).astype(BF16)
+        found = lax.dot_general(
+            tables, picks, (((0,), (0,)), ((), ())), preferred_element_type=F32
+        )
+        found = 128.0 * found[:128] + found[128:]
+        inside = jnp.sum(jnp.where(lane_of == (far & 127), found, 0.0), axis=0, keepdims=True)
         acc = acc + flags_ref[:, start : start + chunk].astype(F32) * inside
-    out_ref[...] = jnp.broadcast_to(jnp.sum(acc, axis=1, keepdims=True), out_ref.shape)
-
-
-def count_cells(valid_bins, offset_limit):
+    counted = jnp.sum(acc, axis=1, keepdims=True) - jnp.sum(
+        jnp.sum(square.astype(F32) * table, axis=1, keepdims=True), axis=0, keepdims=True
+    )
+    count_ref[...] = jnp.broadcast_to(counted, count_ref.shape)
+    flag_line[...] = jnp.zeros(flag_line.shape, F32)
+    limit_line[...] = jnp.zeros(limit_line.shape, F32)
+    flag_line[:, 128 : 128 + total] = flags_ref[...].astype(F32)
+    limit_line[:, 128 : 128 + total] = limit_ref[...].astype(F32)
+
+
+def prep(valid_bins, offset_limit, more):
     total = valid_bins.shape[0]
-    rows = -(-(total // 128 + 1) // 128) * 128
-    flags = jnp.zeros((rows, 128), jnp.int32)
-    flags = lax.dynamic_update_slice(flags, valid_bins.reshape(total // 128, 128), (0, 0))
     return pl.pallas_call(
-        count_body, out_shape=jax.ShapeDtypeStruct((8, 128), F32), name="count"
-    )(valid_bins[None], flags.astype(F32).T, offset_limit[None])
+        prep_body,
+        out_shape=(
+            jax.ShapeDtypeStruct((8, 128), F32),
+            jax.ShapeDtypeStruct((1, 128 + total + more), F32),
+            jax.ShapeDtypeStruct((1, 128 + total + 512), F32),
+        ),
+        name="prep",
+    )(valid_bins[None], valid_bins.reshape(total // 128, 128), offset_limit[None])
 
 
 def band_body(
     info_ref,
     embed_ref,
-    flag_near_ref,
-    flag_far_ref,
+    flag_ref,
     limit_ref,
     target_ref,
     fwd_ref,
@@ -122,10 +129,8 @@
     head_ref,
     count_ref,
     pred_ref,
-    near_out,
-    far_out,
+    sums_out,
     grad_out,
-    err_out,
     lines,
     parts,
     dress,
@@ -133,8 +138,8 @@
     weights,
     goals,
 ):
-    wide = limit_ref.shape[1]
-    chans = near_out.shape[0]
+    wide = goals.shape[1]
+    chans = embed_ref.shape[0] // 2
     cols, rows = pred_ref.shape
     steps = cols + 2 * EDGE
     first_mid, last_mid = HALO, steps - HALO
@@ -155,11 +160,26 @@
         near.astype(BF16),
         moved_left(near, dilation).astype(BF16),
     )
-    flag_near = moved_left(jnp.broadcast_to(flag_near_ref[...], (8, wide)), EDGE)
-    limit = moved_left(jnp.broadcast_to(limit_ref[...], (8, wide)), EDGE)
-    goals[...] = moved_left(target_ref[...], EDGE)
+
+    def around(ref, start):
+        start = pl.multiple_of(start, 128)
+        before = ref[:, pl.ds(start, 128)]
+        body = ref[:, pl.ds(pl.multiple_of(start + 128, 128), wide)]
+        last = jnp.where(lane[:, :128] < turn % 128, body[:, wide - 128 :], before)
+        return jnp.broadcast_to(
+            jnp.concatenate([body[:, : wide - 128], last], axis=1), (8, wide)
+        )
+
+    flag_near = around(flag_ref, row_start)
+    limit = around(limit_ref, row_start)
+    goals[...] = jnp.zeros(goals.shape, F32)
+    goals[:, : target_ref.shape[1]] = target_ref[...].astype(F32)
+    goals[...] = moved_left(goals[...], HALO)
     far = moved_left(embed_ref[chans:].astype(F32), HALO).astype(BF16)
-    flags = moved_left(jnp.broadcast_to(flag_far_ref[...], (8, wide_far)), HALO)
+    flags = flag_ref[:, pl.ds(pl.multiple_of(row_start + offs_start, 128), wide_far + 128)]
+    flags = moved_left(
+        jnp.broadcast_to(flags, (8, wide_far + 128)), 128 - 2 * EDGE + HALO
+    )[:, :wide_far]
     tiles = wide // 128
     tiles_far = wide_far // 128
     lane_tile = lax.broadcasted_iota(jnp.int32, (chans, 128), 1)
@@ -190,11 +210,11 @@
     total_lines = steps + 2 * HALO
     both = total_lines - 128
 
-    @pl.loop(0, both, unroll=8)
+    @pl.loop(0, both, unroll=16)
     def _(shift):
         make_line(shift, 2)
 
-    @pl.loop(both, 128, unroll=8)
+    @pl.loop(both, 128, unroll=16)
     def _(shift):
         make_line(shift, 1)
 
@@ -250,10 +270,10 @@
     err = lax.fori_loop(
         steps - EDGE, last_mid, lambda t, e: make_dres(t, e, False), err, unroll=4
     )
-    err_out[...] = jnp.broadcast_to(jnp.sum(err, axis=1, keepdims=True), err_out.shape)
+    err = jnp.broadcast_to(jnp.sum(err, axis=1, keepdims=True), (1, 128))
     back = back_ref[...]
 
-    @pl.loop(first_mid, last_mid, unroll=36)
+    @pl.loop(first_mid, last_mid, unroll=72)
     def _(t):
         dres = dress[t]
         stacked = jnp.concatenate(
@@ -291,8 +311,11 @@
         make_grads,
         (jnp.zeros((chans, rows), F32), jnp.zeros((chans, wide), F32)),
     )
-    near_out[...] = near_sum
-    far_out[...] = far_sum
+    group, each, _ = sums_out.shape
+    sums_out[...] = jnp.zeros(sums_out.shape, F32)
+    for first in range(0, chans, each):
+        sums_out[first // each, :, :rows] = near_sum[first : first + each]
+        sums_out[(chans + first) // each, :, :wide] = far_sum[first : first + each]
     grad_out[...] = jnp.zeros((3 * chans, 3 * chans), F32)
 
     def add_weight_grads(first, batch):
@@ -314,7 +337,7 @@
             left, right, (((1,), (1,)), ((), ())), preferred_element_type=F32
         )
 
-    batch = 16
+    batch = 32
 
     @pl.loop(0, cols // batch)
     def _(n):
@@ -328,24 +351,31 @@
     def _():
         add_weight_grads(steps - EDGE, HALO)
 
-
-def band(info, embed, flag_near, flag_far, limit, target, fwd, back, head, count, rows, cols):
+    total = grad_out[...]
+    size = 3 * chans
+    for index in range(group):
+        first = 3 * index
+        sums_out[index, 0:1, wide : wide + size] = total[first : first + 1]
+        sums_out[index, 0:1, wide + 128 : wide + 128 + size] = total[first + 1 : first + 2]
+        sums_out[index, 1:2, wide : wide + size] = total[first + 2 : first + 3]
+        sums_out[index, 1:2, wide + 128 :] = err
+
+
+def band(info, embed, flag_line, limit_line, target, fwd, back, head, count, rows, cols, group):
     chans = embed.shape[0] // 2
-    wide = limit.shape[1]
+    wide = 512
     steps = cols + 2 * EDGE
     vmem = pl.BlockSpec(memory_space=pltpu.VMEM)
     return pl.pallas_call(
         band_body,
         out_shape=(
             jax.ShapeDtypeStruct((cols, rows), F32),
-            jax.ShapeDtypeStruct((chans, rows), F32),
-            jax.ShapeDtypeStruct((chans, wide), F32),
-            jax.ShapeDtypeStruct((3 * chans, 3 * chans), F32),
-            jax.ShapeDtypeStruct((8, 128), F32),
+            jax.ShapeDtypeStruct((group, 2 * chans // group, wide + 256), F32),
         ),
-        in_specs=[pl.BlockSpec(memory_space=pltpu.SMEM)] + [vmem] * 9,
-        out_specs=(vmem,) * 5,
+        in_specs=[pl.BlockSpec(memory_space=pltpu.SMEM)] + [vmem] * 8,
+        out_specs=(vmem,) * 2,
         scratch_shapes=[
+            pltpu.VMEM((3 * chans, 3 * chans), F32),
             pltpu.VMEM((steps + 2 * HALO, chans, wide), BF16),
             pltpu.VMEM((steps, 3 * chans, wide), F32),
             pltpu.VMEM((steps, chans, wide), BF16),
@@ -355,11 +385,11 @@
         ],
         compiler_params=pltpu.CompilerParams(vmem_limit_bytes=60 * 1024 * 1024),
         name="band",
-    )(info, embed, flag_near, flag_far, limit, target, fwd, back, head, count)
+    )(info, embed, flag_line, limit_line, target, fwd, back, head, count)
 
 
 def place(info_ref, b, o, rows, cols):
-    return pl.multiple_of(b * rows + info_ref[0] * (info_ref[1] + o * cols), 128)
+    return pl.multiple_of(b * rows + info_ref[5] * (info_ref[6] + o * cols), 128)
 
 
 def windows_body(n_off, rows, cols, info_ref, tiles_ref, out_ref, line):
@@ -456,8 +486,26 @@
     framed = with_halo(activ, "enc", 1, HALO)
     framed_bins = encoder_bins + 2 * HALO
     everywhere = from_everyone(framed, GROUP).reshape(width_in, framed_bins)
-    count = count_cells(valid_bins, offset_limit)
-    goal = with_halo(target.T, "bin", 1, HALO)
+    wide = 512
+    wide_far = 640
+    count, flag_line, limit_line = prep(valid_bins, offset_limit, extent + wide_far)
+    is_far = (bin_id * n_off + off_id) * each >= second
+    values = (
+        second_dilation,
+        offs_start,
+        row_start,
+        extent,
+        length,
+        is_far.astype(jnp.int32),
+        enc_id * n_off * cols,
+    )
+    slot = jnp.arange(8, dtype=jnp.int32)
+    info = sum(jnp.where(slot == index, value, 0) for index, value in enumerate(values))
+    info = info.astype(jnp.int32)
+    goal = with_halo(target, "bin", 0, HALO).T
+    everywhere, goal, count, flag_line, limit_line, info = lax.optimization_barrier(
+        (everywhere, goal, count, flag_line, limit_line, info)
+    )
     goal = with_halo(goal, ("enc", "off"), 0, HALO)
 
     weight_one = conv_one.reshape(3 * chans, width_in)
@@ -471,32 +519,20 @@
     hidden = (encoder_in.astype(F32) + conv_out).astype(BF16)
     proj_rows = jnp.transpose(proj_weight, (0, 2, 1)).reshape(2 * second, chans)
     partial_embed = jnp.dot(proj_rows, hidden, preferred_element_type=F32)
-    summed = exchange(partial_embed.reshape(group, each, encoder_bins), GROUP).sum(axis=0)
+    summed = exchange(partial_embed.reshape(group, each, encoder_bins), GROUP)
+    summed = summed.sum(axis=0)
     tiles = from_everyone(summed.astype(BF16), "enc")
-    wide = 512
-    wide_far = 640
-    is_far = (bin_id * n_off + off_id) * each >= second
-    spots = jnp.stack([is_far.astype(jnp.int32), enc_id * n_off * cols]).astype(jnp.int32)
-    embed = exchange(windows(spots, tiles, n_bin, n_off, rows, cols, wide_far), GROUP)
+    tiles, conv_two, head_weight = lax.optimization_barrier((tiles, conv_two, head_weight))
+    embed = exchange(windows(info, tiles, n_bin, n_off, rows, cols, wide_far), GROUP)
     embed = embed.reshape(2 * second, wide_far)
-    flags = jnp.pad(valid_bins.astype(F32), (2 * EDGE, extent + wide_far))[None]
-    flag_near = lax.dynamic_slice_in_dim(flags, row_start + EDGE, wide, 1)
-    flag_far = lax.dynamic_slice_in_dim(flags, row_start + offs_start, wide_far, 1)
-    limits = jnp.pad(offset_limit.astype(F32), (EDGE, wide))[None]
-    limit = lax.dynamic_slice_in_dim(limits, row_start, wide, 1)
-    goal = jnp.pad(goal.astype(F32), ((0, 0), (HALO, wide - rows - 3 * HALO)))
-    info = jnp.stack(
-        [second_dilation, offs_start, row_start, jnp.int32(extent), jnp.int32(length)]
-    ).astype(jnp.int32)
     taps_two = conv_two.reshape(3, 3, second, second)
     fwd = jnp.transpose(taps_two, (1, 3, 0, 2)).reshape(3 * second, 3 * second)
     back = jnp.transpose(taps_two, (1, 2, 0, 3)).reshape(3 * second, 3 * second)
-    pred, near_grad, far_grad, band_grad, error = band(
+    pred, parts = band(
         info,
         embed,
-        flag_near,
-        flag_far,
-        limit,
+        flag_line,
+        limit_line,
         goal,
         fwd,
         back,
@@ -504,22 +540,12 @@
         count,
         rows,
         cols,
+        group,
     )
     prediction = pred.T
 
-    size = 9 * second * second
-    share = size // group
-    pad_share = -(-(share + 1) // (each * 128)) * 128
-    extra = jnp.concatenate(
-        [band_grad.reshape(group, share), jnp.broadcast_to(error[0:1, 0:1], (group, 1))], axis=1
-    )
-    extra = jnp.pad(extra, ((0, 0), (0, each * pad_share - share - 1)))
-    parts = jnp.concatenate(
-        [jnp.pad(near_grad, ((0, 0), (0, wide - rows))), far_grad], axis=0
-    ).reshape(group, each, wide)
-    parts = jnp.concatenate([parts, extra.reshape(group, each, pad_share)], axis=2)
     parts = lines_of(
-        spots, exchange(parts, GROUP), n_enc, n_off, encoder_bins, rows, cols, wide
+        info, exchange(parts, GROUP), n_enc, n_off, encoder_bins, rows, cols, wide
     )
     parts = exchange(parts, "enc").sum(axis=0)
     grad_embed = parts[:, :encoder_bins].astype(BF16).astype(F32)
@@ -527,14 +553,17 @@
         jnp.concatenate([grad_embed, parts[:, encoder_bins:]], axis=1), GROUP
     )
     grad_rows = gathered[:, :, :encoder_bins].reshape(2 * second, encoder_bins).astype(BF16)
-    extra = gathered[:, :, encoder_bins:].reshape(group, each * pad_share)
+    extra = gathered[:, :, encoder_bins:]
+    grad_conv_two = jnp.stack(
+        [extra[:, 0, : 3 * second], extra[:, 0, 128 : 128 + 3 * second], extra[:, 1, : 3 * second]],
+        axis=1,
+    )
     grad_conv_two = (
-        extra[:, :share]
-        .reshape(3, second, 3, second)
+        grad_conv_two.reshape(3, second, 3, second)
         .transpose(0, 2, 1, 3)
         .reshape(9, second, second)
     )
-    loss_mean = extra[0, share : share + 1] / (1.0 + count[0, 0:1])
+    loss_mean = extra[0, 1, 128:129] / (1.0 + count[0, 0:1])
 
     dhidden = jnp.dot(proj_rows.T, grad_rows, preferred_element_type=F32).astype(BF16)
     proj_local = lax.dot_general(

time: 177 us -> 169 us (0.955)
  local copies, waits for them, and re-layouts: 22.3 us -> 15.4 us
  waiting for transfers between devices: 17.1 us -> 22.1 us
  Pallas kernels: 34.4 us -> 31.2 us
  starting transfers between devices: 49.7 us -> 47.1 us
    all_to_all x5, waiting for transfers between devices: 15.8 us -> 20.8 us  [exchange(): return lax.all_to_all(array, axis, 0, 0, tiled=True)]
    all_to_all x5, starting transfers between devices: 33.7 us -> 31.1 us  [exchange(): return lax.all_to_all(array, axis, 0, 0, tiled=True)]
    another operation x6 -> x2, local copies, waits for them, and re-layouts: 2.59 us -> 0.01 us
    unnamed x29 -> x20, local copies, waits for them, and re-layouts: 5.5 us -> 3.52 us
  transfers between devices with their start and end apart: 11 -> 11, of which waited for: 5 -> 6; matrix products, arithmetic and copies ran while one was open for 8% -> 5% of each run, Pallas kernels for 3% -> 3%
where the time goes in v2:
time: 169 us; the launch traced here: 168 us
  starting transfers between devices  47.1 us (28%)
  blocking collectives  41.6 us (25%)
  Pallas kernels  31.2 us (18%)
  waiting for transfers between devices  22.1 us (13%)
  local copies, waits for them, and re-layouts  15.4 us (9%)
  between operations  5.44 us (3%)
  other arithmetic  3.81 us (2%)
    all_to_all x3, blocking collectives, exchange(): return lax.all_to_all(array, axis, 0, 0, tiled=True)  41.6 us
    all_to_all x5, starting transfers between devices, exchange(): return lax.all_to_all(array, axis, 0, 0, tiled=True)  31.1 us
    pallas_call x1, Pallas kernels, band(): pl.pallas_call(band_body, out_shape=(jax.ShapeDtypeStruct((cols, rows), F...  25 us
    all_to_all x5, waiting for transfers between devices, exchange(): return lax.all_to_all(array, axis, 0, 0, tiled=True)  20.8 us
    ppermute x3, starting transfers between devices, with_halo(): lax.ppermute(tail, axis, [(i, (i + 1) % count) for i in range(ends)])  11.4 us
    ppermute x3, starting transfers between devices, with_halo(): lax.ppermute(head, axis, [((i + 1) % count, i) for i in range(ends)])  4.59 us
    unnamed x20, local copies, waits for them, and re-layouts  3.52 us
  transfers between devices with their start and end apart: 11, of which 6 were waited for; matrix products, arithmetic and copies ran while one was open for 5% of the time, Pallas kernels for 3%

profile of v2, /device:TPU:2, one launch (start us, length us, event | category | flops | bytes accessed | tf_op | source)
XLA Modules:
  0.0 167.8 jit_solution(10158606491599158706)
XLA Ops:
  0.6 0.8 fusion.14
  1.6 1.3 collective-permute-start.1
  2.9 4.5 %collective-permute-start = (bf16[16,8]{1,0:T(8,128)(2,1)S(1)}, bf16[16,8]{1,0:T(8,128)(2,1)S(1)}, u32[]{:S(2)}, u32[]{:S(2)}) collective-permute-start(bf16[16,8]{1,0:T(8,128)(2,1)S(1)} %get-tuple-element.55), channel_id=1, source_target_pairs={{0,32},{32,64},{64,96},{96,128},{128,160},{160,192},{192,224},{1,3... | collective-permute-start | bytes 776 | tf_op jit(solution)/shard_map/ppermute | solution.py:25
  7.4 1.3 collective-permute-done
  8.8 1.0 broadcast_in_dim.67
  9.8 7.8 %all-to-all-start = ((bf16[32,16,784]{2,1,0:T(8,128)(2,1)}), bf16[32,16,784]{2,1,0:T(8,128)(2,1)S(1)}, u32[]{:S(2)}, u32[]{:S(2)}) async-start(bf16[32,16,784]{2,1,0:T(8,128)(2,1)} %broadcast_in_dim.67), calls=%async_computation | async-start | bytes 1835008 | tf_op jit(solution)/shard_map/all_to_all | solution.py:34
  17.7 2.0 %collective-permute-start.3 = (bf16[8,128]{0,1:T(8,128)(2,1)S(1)}, bf16[8,128]{0,1:T(8,128)(2,1)S(1)}, u32[]{:S(2)}, u32[]{:S(2)}) collective-permute-start(bf16[8,128]{0,1:T(8,128)(2,1)S(1)} %copy.33), channel_id=1, source_target_pairs={{2,0},{4,2},{6,4},{8,6},{10,8},{12,10},{14,12},{16,14},{18,16},{20... | collective-permute-start | bytes 6152 | tf_op jit(solution)/shard_map/ppermute | solution.py:27
  19.9 2.3 %collective-permute-start.2 = (bf16[8,128]{0,1:T(8,128)(2,1)S(1)}, bf16[8,128]{0,1:T(8,128)(2,1)S(1)}, u32[]{:S(2)}, u32[]{:S(2)}) collective-permute-start(bf16[8,128]{0,1:T(8,128)(2,1)S(1)} %copy.32), channel_id=1, source_target_pairs={{0,2},{2,4},{4,6},{6,8},{8,10},{10,12},{12,14},{14,16},{16,18},{18... | collective-permute-start | bytes 6152 | tf_op jit(solution)/shard_map/ppermute | solution.py:25
  22.2 0.6 copy-done.7
  22.8 0.6 fusion.39
  23.4 1.1 fusion.30.refs_0_.info_ref
  26.8 2.9 %prep.1 = (f32[8,128]{1,0:T(8,128)}, f32[1,8960]{1,0:T(1,128)}, f32[1,6784]{1,0:T(1,128)}) custom-call(s32[1,6144]{1,0:T(1,128)} %bitcast.63, s32[48,128]{1,0:T(8,128)} %bitcast.64, s32[1,6144]{1,0:T(1,128)} %bitcast.65), custom_call_target="tpu_custom_call" | custom-call | tf_op jit(solution)/shard_map/prep/pallas_call | solution.py:110
  29.8 3.2 %all-to-all-done = bf16[32,16,784]{2,1,0:T(8,128)(2,1)S(1)} async-done(((bf16[32,16,784]{2,1,0:T(8,128)(2,1)}), bf16[32,16,784]{2,1,0:T(8,128)(2,1)S(1)}, u32[]{:S(2)}, u32[]{:S(2)}) %all-to-all-start) | async-done | bytes 802848 | tf_op jit(solution)/shard_map/all_to_all | solution.py:34
  33.3 0.5 copy-done.4
  34.2 14.5 %all_to_all.40 = f32[32,2,768]{2,1,0:T(2,128)S(1)} all-to-all(f32[32,2,768]{2,1,0:T(2,128)S(1)} %reshape.84), channel_id=1, replica_groups=mesh['enc'=8,'bin'=16,'off'=2] {'bin','off'}, dimensions={0} | all-to-all | bytes 393216 | tf_op jit(solution)/shard_map/all_to_all | solution.py:34
  48.8 0.6 broadcast_in_dim.77
  49.4 10.0 %all-to-all-start.2 = ((bf16[8,2,768]{2,1,0:T(2,128)(2,1)}), bf16[8,2,768]{2,1,0:T(2,128)(2,1)S(1)}, u32[]{:S(2)}, u32[]{:S(2)}) async-start(bf16[8,2,768]{2,1,0:T(2,128)(2,1)} %broadcast_in_dim.77), calls=%async_computation.2 | async-start | bytes 49152 | tf_op jit(solution)/shard_map/all_to_all | solution.py:34
  59.4 1.3 collective-permute-start.5
  60.7 4.5 %collective-permute-start.4 = (bf16[8,400]{1,0:T(8,128)(2,1)S(1)}, bf16[8,400]{1,0:T(8,128)(2,1)S(1)}, u32[]{:S(2)}, u32[]{:S(2)}) collective-permute-start(bf16[8,400]{1,0:T(8,128)(2,1)S(1)} %get-tuple-element.51), channel_id=1, source_target_pairs={{0,1},{1,32},{32,33},{33,64},{64,65},{65,96},{96,97},{97,128},{128... | collective-permute-start | bytes 19208 | tf_op jit(solution)/shard_map/ppermute | solution.py:25
  65.3 2.0 %all-to-all-done.2.refs_1_ = bf16[8,2,768]{2,1,0:T(2,128)(2,1)S(1)} async-done(((bf16[8,2,768]{2,1,0:T(2,128)(2,1)}), bf16[8,2,768]{2,1,0:T(2,128)(2,1)S(1)}, u32[]{:S(2)}, u32[]{:S(2)}) %all-to-all-start.2) | async-done | bytes 24608 | tf_op jit(solution)/shard_map/all_to_all | solution.py:34
  67.2 0.6 copy-done.5
  67.9 1.6 windows.1
  69.4 4.9 %all-to-all-start.3 = ((bf16[32,2,640]{2,1,0:T(2,128)(2,1)}), bf16[32,2,640]{2,1,0:T(2,128)(2,1)S(1)}, u32[]{:S(2)}, u32[]{:S(2)}) async-start(bf16[32,2,640]{2,1,0:T(2,128)(2,1)} %windows.1), calls=%async_computation.3 | async-start | bytes 163840 | tf_op jit(solution)/shard_map/all_to_all | solution.py:34
  74.4 0.7 pad_maximum_fusion.target_ref
  75.4 0.7 reshape.87.fwd_ref
  76.1 0.7 reshape.88.back_ref
  76.8 0.7 copy-done.8
  77.5 0.7 copy.38.head_ref
  78.2 2.9 %all-to-all-done.3 = bf16[32,2,640]{2,1,0:T(2,128)(2,1)S(1)} async-done(((bf16[32,2,640]{2,1,0:T(2,128)(2,1)}), bf16[32,2,640]{2,1,0:T(2,128)(2,1)S(1)}, u32[]{:S(2)}, u32[]{:S(2)}) %all-to-all-start.3) | async-done | bytes 81952 | tf_op jit(solution)/shard_map/all_to_all | solution.py:34
  81.0 0.7 reshape.85.embed_ref
  81.7 25.0 %band.1 = (f32[128,384]{1,0:T(8,128)}, f32[32,2,768]{2,1,0:T(2,128)}) custom-call(s32[8]{0:T(128)} %fusion.30.refs_0_.info_ref, bf16[64,640]{1,0:T(8,128)(2,1)} %reshape.85.embed_ref, f32[1,8960]{1,0:T(1,128)} %get-tuple-element.25.flag_ref, f32[1,6784]{1,0:T(1,128)} %get-tuple-element.26.limit_ref, bf16[144,400]{1,0:T(8,128)(2,1)} %pad_maximum_fusion.target_ref, ...), custom_call_target="tpu_custom_call" | custom-call | tf_op jit(solution)/shard_map/band/pallas_call | solution.py:369
  106.7 13.4 %all_to_all.41.refs_1_ = f32[32,2,768]{2,1,0:T(2,128)} all-to-all(f32[32,2,768]{2,1,0:T(2,128)} %get-tuple-element.32), channel_id=1, replica_groups=mesh['enc'=8,'bin'=16,'off'=2] {'bin','off'}, dimensions={0} | all-to-all | bytes 393216 | tf_op jit(solution)/shard_map/all_to_all | solution.py:34
  120.1 1.8 %lines.1 = f32[8,2,1024]{2,1,0:T(2,128)} custom-call(s32[8]{0:T(128)} %fusion.30.refs_0_.info_ref, f32[32,2,768]{2,1,0:T(2,128)} %all_to_all.41.refs_1_), custom_call_target="tpu_custom_call" | custom-call | tf_op jit(solution)/shard_map/lines/pallas_call | solution.py:442
  121.9 13.7 %all_to_all.42 = f32[8,2,1024]{2,1,0:T(2,128)S(1)} all-to-all(f32[8,2,1024]{2,1,0:T(2,128)} %lines.1), channel_id=1, replica_groups=mesh['enc'=8,'bin'=16,'off'=2] {'enc'}, dimensions={0} | all-to-all | bytes 131072 | tf_op jit(solution)/shard_map/all_to_all | solution.py:34
  135.7 0.8 broadcast_in_dim.79
  136.5 5.0 %all-to-all-start.6 = ((f32[32,2,1024]{2,1,0:T(2,128)}), f32[32,2,1024]{2,1,0:T(2,128)S(1)}, u32[]{:S(2)}, u32[]{:S(2)}) async-start(f32[32,2,1024]{2,1,0:T(2,128)} %broadcast_in_dim.79), calls=%async_computation.6 | async-start | bytes 524288 | tf_op jit(solution)/shard_map/all_to_all | solution.py:34
  141.5 1.2 slice.71
  143.4 0.8 copy.41
  144.2 5.8 %all-to-all-done.6 = f32[32,2,1024]{2,1,0:T(2,128)S(1)} async-done(((f32[32,2,1024]{2,1,0:T(2,128)}), f32[32,2,1024]{2,1,0:T(2,128)S(1)}, u32[]{:S(2)}, u32[]{:S(2)}) %all-to-all-start.6) | async-done | bytes 262176 | tf_op jit(solution)/shard_map/all_to_all | solution.py:34
  150.6 0.5 dynamic_update_slice.11
  151.1 0.5 dynamic_update_slice.9
  152.2 0.7 pad_maximum_fusion.1
  152.9 3.4 %all-to-all-start.7 = ((f32[8,32,128]{2,1,0:T(8,128)}), f32[8,32,128]{2,1,0:T(8,128)S(1)}, u32[]{:S(2)}, u32[]{:S(2)}) async-start(f32[8,32,128]{2,1,0:T(8,128)} %pad_maximum_fusion.1), calls=%async_computation.7 | async-start | bytes 262144 | tf_op jit(solution)/shard_map/all_to_all | solution.py:34
  156.5 0.7 copy.39
  157.2 0.5 slice.82
  158.4 6.9 %all-to-all-done.7 = f32[8,32,128]{2,1,0:T(8,128)S(1)} async-done(((f32[8,32,128]{2,1,0:T(8,128)}), f32[8,32,128]{2,1,0:T(8,128)S(1)}, u32[]{:S(2)}, u32[]{:S(2)}) %all-to-all-start.7) | async-done | bytes 131104 | tf_op jit(solution)/shard_map/all_to_all | solution.py:34
  165.3 0.7 reshape.93
  166.0 0.7 reshape.94
  (59 shorter events, 3.4 us)
Async XLA Ops:
  0.6 32.4 %copy-start = (bf16[3,16,512]{2,1,0:T(8,128)(2,1)S(1)}, bf16[3,16,512]{2,1,0:T(8,128)(2,1)}, u32[]{:S(2)}) copy-start(bf16[3,16,512]{2,1,0:T(8,128)(2,1)} %param.12) | copy-start | bytes 147460
  1.6 5.8 %collective-permute-start.1 = (bf16[16,8]{1,0:T(8,128)(2,1)S(1)}, bf16[16,8]{1,0:T(8,128)(2,1)S(1)}, u32[]{:S(2)}, u32[]{:S(2)}) collective-permute-start(bf16[16,8]{1,0:T(8,128)(2,1)S(1)} %get-tuple-element.56), channel_id=1, source_target_pairs={{32,0},{64,32},{96,64},{128,96},{160,128},{192,160},{224,192},{33,... | collective-permute-start | bytes 776 | tf_op jit(solution)/shard_map/ppermute | solution.py:27
  2.9 5.9 %collective-permute-start = (bf16[16,8]{1,0:T(8,128)(2,1)S(1)}, bf16[16,8]{1,0:T(8,128)(2,1)S(1)}, u32[]{:S(2)}, u32[]{:S(2)}) collective-permute-start(bf16[16,8]{1,0:T(8,128)(2,1)S(1)} %get-tuple-element.55), channel_id=1, source_target_pairs={{0,32},{32,64},{64,96},{96,128},{128,160},{160,192},{192,224},{1,3... | collective-permute-start | bytes 776 | tf_op jit(solution)/shard_map/ppermute | solution.py:25
  9.8 7.8 %copy-start.3 = (bf16[384,128]{1,0:T(8,128)(2,1)S(1)}, bf16[384,128]{1,0:T(8,128)(2,1)}, u32[]{:S(2)}) copy-start(bf16[384,128]{1,0:T(8,128)(2,1)} %param.16) | copy-start | bytes 294916
  9.8 23.2 %all-to-all-start = ((bf16[32,16,784]{2,1,0:T(8,128)(2,1)}), bf16[32,16,784]{2,1,0:T(8,128)(2,1)S(1)}, u32[]{:S(2)}, u32[]{:S(2)}) async-start(bf16[32,16,784]{2,1,0:T(8,128)(2,1)} %broadcast_in_dim.67), calls=%async_computation | async-start | bytes 1835008 | tf_op jit(solution)/shard_map/all_to_all | solution.py:34
  17.7 11.9 %collective-permute-start.3 = (bf16[8,128]{0,1:T(8,128)(2,1)S(1)}, bf16[8,128]{0,1:T(8,128)(2,1)S(1)}, u32[]{:S(2)}, u32[]{:S(2)}) collective-permute-start(bf16[8,128]{0,1:T(8,128)(2,1)S(1)} %copy.33), channel_id=1, source_target_pairs={{2,0},{4,2},{6,4},{8,6},{10,8},{12,10},{14,12},{16,14},{18,16},{20... | collective-permute-start | bytes 6152 | tf_op jit(solution)/shard_map/ppermute | solution.py:27
  19.9 9.8 %collective-permute-start.2 = (bf16[8,128]{0,1:T(8,128)(2,1)S(1)}, bf16[8,128]{0,1:T(8,128)(2,1)S(1)}, u32[]{:S(2)}, u32[]{:S(2)}) collective-permute-start(bf16[8,128]{0,1:T(8,128)(2,1)S(1)} %copy.32), channel_id=1, source_target_pairs={{0,2},{2,4},{4,6},{6,8},{8,10},{10,12},{12,14},{14,16},{16,18},{18... | collective-permute-start | bytes 6152 | tf_op jit(solution)/shard_map/ppermute | solution.py:25
  22.2 0.7 copy-start.7
  26.0 0.7 copy-start.6
  33.0 0.7 copy-start.4
  49.4 17.9 %all-to-all-start.2 = ((bf16[8,2,768]{2,1,0:T(2,128)(2,1)}), bf16[8,2,768]{2,1,0:T(2,128)(2,1)S(1)}, u32[]{:S(2)}, u32[]{:S(2)}) async-start(bf16[8,2,768]{2,1,0:T(2,128)(2,1)} %broadcast_in_dim.77), calls=%async_computation.2 | async-start | bytes 49152 | tf_op jit(solution)/shard_map/all_to_all | solution.py:34
  59.4 14.9 %collective-permute-start.5 = (bf16[8,400]{1,0:T(8,128)(2,1)S(1)}, bf16[8,400]{1,0:T(8,128)(2,1)S(1)}, u32[]{:S(2)}, u32[]{:S(2)}) collective-permute-start(bf16[8,400]{1,0:T(8,128)(2,1)S(1)} %get-tuple-element.52), channel_id=1, source_target_pairs={{1,0},{32,1},{33,32},{64,33},{65,64},{96,65},{97,96},{128,97},{129... | collective-permute-start | bytes 19208 | tf_op jit(solution)/shard_map/ppermute | solution.py:27
  60.7 13.6 %collective-permute-start.4 = (bf16[8,400]{1,0:T(8,128)(2,1)S(1)}, bf16[8,400]{1,0:T(8,128)(2,1)S(1)}, u32[]{:S(2)}, u32[]{:S(2)}) collective-permute-start(bf16[8,400]{1,0:T(8,128)(2,1)S(1)} %get-tuple-element.51), channel_id=1, source_target_pairs={{0,1},{1,32},{32,33},{33,64},{64,65},{65,96},{96,97},{97,128},{128... | collective-permute-start | bytes 19208 | tf_op jit(solution)/shard_map/ppermute | solution.py:25
  67.2 0.6 copy-start.5
  69.4 11.6 %all-to-all-start.3 = ((bf16[32,2,640]{2,1,0:T(2,128)(2,1)}), bf16[32,2,640]{2,1,0:T(2,128)(2,1)S(1)}, u32[]{:S(2)}, u32[]{:S(2)}) async-start(bf16[32,2,640]{2,1,0:T(2,128)(2,1)} %windows.1), calls=%async_computation.3 | async-start | bytes 163840 | tf_op jit(solution)/shard_map/all_to_all | solution.py:34
  74.3 0.9 copy-start.1
  76.8 0.7 copy-start.8
  136.4 6.9 %copy-start.2 = (f32[128,384]{1,0:T(8,128)S(1)}, f32[128,384]{1,0:T(8,128)}, u32[]{:S(2)}) copy-start(f32[128,384]{1,0:T(8,128)} %get-tuple-element.31) | copy-start | bytes 589828
  136.5 13.6 %all-to-all-start.6 = ((f32[32,2,1024]{2,1,0:T(2,128)}), f32[32,2,1024]{2,1,0:T(2,128)S(1)}, u32[]{:S(2)}, u32[]{:S(2)}) async-start(f32[32,2,1024]{2,1,0:T(2,128)} %broadcast_in_dim.79), calls=%async_computation.6 | async-start | bytes 524288 | tf_op jit(solution)/shard_map/all_to_all | solution.py:34
  152.9 12.4 %all-to-all-start.7 = ((f32[8,32,128]{2,1,0:T(8,128)}), f32[8,32,128]{2,1,0:T(8,128)S(1)}, u32[]{:S(2)}, u32[]{:S(2)}) async-start(f32[8,32,128]{2,1,0:T(8,128)} %pad_maximum_fusion.1), calls=%async_computation.7 | async-start | bytes 262144 | tf_op jit(solution)/shard_map/all_to_all | solution.py:34

commit v3 on v2

--- a/solution.py
+++ b/solution.py
@@ -503,10 +503,7 @@
     info = sum(jnp.where(slot == index, value, 0) for index, value in enumerate(values))
     info = info.astype(jnp.int32)
     goal = with_halo(target, "bin", 0, HALO).T
-    everywhere, goal, count, flag_line, limit_line, info = lax.optimization_barrier(
-        (everywhere, goal, count, flag_line, limit_line, info)
-    )
-    goal = with_halo(goal, ("enc", "off"), 0, HALO)
+    everywhere, goal = lax.optimization_barrier((everywhere, goal))
 
     weight_one = conv_one.reshape(3 * chans, width_in)
     taps = jnp.dot(weight_one, everywhere, preferred_element_type=F32)
@@ -520,6 +517,10 @@
     proj_rows = jnp.transpose(proj_weight, (0, 2, 1)).reshape(2 * second, chans)
     partial_embed = jnp.dot(proj_rows, hidden, preferred_element_type=F32)
     summed = exchange(partial_embed.reshape(group, each, encoder_bins), GROUP)
+    summed, goal, count, flag_line, limit_line, info = lax.optimization_barrier(
+        (summed, goal, count, flag_line, limit_line, info)
+    )
+    goal = with_halo(goal, ("enc", "off"), 0, HALO)
     summed = summed.sum(axis=0)
     tiles = from_everyone(summed.astype(BF16), "enc")
     tiles, conv_two, head_weight = lax.optimization_barrier((tiles, conv_two, head_weight))

time: 169 us -> 168 us (level)
  blocking collectives: 41.6 us -> 27.1 us
  waiting for transfers between devices: 22.1 us -> 30.5 us
  starting transfers between devices: 47.1 us -> 52 us
    all_to_all x3 -> x2, blocking collectives: 41.6 us -> 27.1 us  [exchange(): return lax.all_to_all(array, axis, 0, 0, tiled=True)]
    all_to_all x5 -> x6, starting transfers between devices: 31.1 us -> 36 us  [exchange(): return lax.all_to_all(array, axis, 0, 0, tiled=True)]
    all_to_all x5 -> x6, waiting for transfers between devices: 20.8 us -> 24.9 us  [exchange(): return lax.all_to_all(array, axis, 0, 0, tiled=True)]
    ppermute x3, waiting for transfers between devices: 0.01 us -> 3.36 us  [with_halo(): lax.ppermute(head, axis, [((i + 1) % count, i) for i in range(ends)])]
  transfers between devices with their start and end apart: 11 -> 12, of which waited for: 6 -> 9; matrix products, arithmetic and copies ran while one was open for 5% -> 5% of each run, Pallas kernels for 3% -> 3%
where the time goes in v3:
time: 168 us; the launch traced here: 167 us
  starting transfers between devices  52 us (31%)
  Pallas kernels  31.2 us (19%)
  waiting for transfers between devices  30.5 us (18%)
  blocking collectives  27.1 us (16%)
  local copies, waits for them, and re-layouts  15.4 us (9%)
  between operations  5.45 us (3%)
  other arithmetic  3.9 us (2%)
    all_to_all x6, starting transfers between devices, exchange(): return lax.all_to_all(array, axis, 0, 0, tiled=True)  36 us
    all_to_all x2, blocking collectives, exchange(): return lax.all_to_all(array, axis, 0, 0, tiled=True)  27.1 us
    pallas_call x1, Pallas kernels, band(): pl.pallas_call(band_body, out_shape=(jax.ShapeDtypeStruct((cols, rows), F...  25 us
    all_to_all x6, waiting for transfers between devices, exchange(): return lax.all_to_all(array, axis, 0, 0, tiled=True)  24.9 us
    ppermute x3, starting transfers between devices, with_halo(): lax.ppermute(tail, axis, [(i, (i + 1) % count) for i in range(ends)])  11.4 us
    ppermute x3, starting transfers between devices, with_halo(): lax.ppermute(head, axis, [((i + 1) % count, i) for i in range(ends)])  4.59 us
    ppermute x3, waiting for transfers between devices, with_halo(): lax.ppermute(head, axis, [((i + 1) % count, i) for i in range(ends)])  3.36 us
  transfers between devices with their start and end apart: 12, of which 9 were waited for; matrix products, arithmetic and copies ran while one was open for 5% of the time, Pallas kernels for 3%

profile of v3, /device:TPU:2, one launch (start us, length us, event | category | flops | bytes accessed | tf_op | source)
XLA Modules:
  0.0 166.8 jit_solution(11241306109420273270)
XLA Ops:
  0.6 0.8 fusion.14
  1.6 1.3 collective-permute-start.1
  2.9 4.5 %collective-permute-start = (bf16[16,8]{1,0:T(8,128)(2,1)S(1)}, bf16[16,8]{1,0:T(8,128)(2,1)S(1)}, u32[]{:S(2)}, u32[]{:S(2)}) collective-permute-start(bf16[16,8]{1,0:T(8,128)(2,1)S(1)} %get-tuple-element.59), channel_id=1, source_target_pairs={{0,32},{32,64},{64,96},{96,128},{128,160},{160,192},{192,224},{1,3... | collective-permute-start | bytes 776 | tf_op jit(solution)/shard_map/ppermute | solution.py:25
  7.4 1.3 collective-permute-done
  8.8 1.0 broadcast_in_dim.67
  9.8 7.8 %all-to-all-start = ((bf16[32,16,784]{2,1,0:T(8,128)(2,1)}), bf16[32,16,784]{2,1,0:T(8,128)(2,1)S(1)}, u32[]{:S(2)}, u32[]{:S(2)}) async-start(bf16[32,16,784]{2,1,0:T(8,128)(2,1)} %broadcast_in_dim.67), calls=%async_computation | async-start | bytes 1835008 | tf_op jit(solution)/shard_map/all_to_all | solution.py:34
  17.7 2.0 %collective-permute-start.3 = (bf16[8,128]{0,1:T(8,128)(2,1)S(1)}, bf16[8,128]{0,1:T(8,128)(2,1)S(1)}, u32[]{:S(2)}, u32[]{:S(2)}) collective-permute-start(bf16[8,128]{0,1:T(8,128)(2,1)S(1)} %copy.33), channel_id=1, source_target_pairs={{2,0},{4,2},{6,4},{8,6},{10,8},{12,10},{14,12},{16,14},{18,16},{20... | collective-permute-start | bytes 6152 | tf_op jit(solution)/shard_map/ppermute | solution.py:27
  19.9 2.3 %collective-permute-start.2 = (bf16[8,128]{0,1:T(8,128)(2,1)S(1)}, bf16[8,128]{0,1:T(8,128)(2,1)S(1)}, u32[]{:S(2)}, u32[]{:S(2)}) collective-permute-start(bf16[8,128]{0,1:T(8,128)(2,1)S(1)} %copy.32), channel_id=1, source_target_pairs={{0,2},{2,4},{4,6},{6,8},{8,10},{10,12},{12,14},{14,16},{16,18},{18... | collective-permute-start | bytes 6152 | tf_op jit(solution)/shard_map/ppermute | solution.py:25
  22.2 0.6 fusion.39
  25.0 3.4 %collective-permute-done.3 = bf16[8,128]{0,1:T(8,128)(2,1)S(1)} collective-permute-done((bf16[8,128]{0,1:T(8,128)(2,1)S(1)}, bf16[8,128]{0,1:T(8,128)(2,1)S(1)}, u32[]{:S(2)}, u32[]{:S(2)}) %collective-permute-start.3) | collective-permute-done | bytes 2080 | tf_op jit(solution)/shard_map/ppermute | solution.py:27
  28.4 0.8 collective-permute-done.2
  29.3 3.7 %all-to-all-done = bf16[32,16,784]{2,1,0:T(8,128)(2,1)S(1)} async-done(((bf16[32,16,784]{2,1,0:T(8,128)(2,1)}), bf16[32,16,784]{2,1,0:T(8,128)(2,1)S(1)}, u32[]{:S(2)}, u32[]{:S(2)}) %all-to-all-start) | async-done | bytes 802848 | tf_op jit(solution)/shard_map/all_to_all | solution.py:34
  34.1 0.8 reshape.83
  34.9 4.9 %all-to-all-start.1 = ((f32[32,2,768]{2,1,0:T(2,128)}), f32[32,2,768]{2,1,0:T(2,128)S(1)}, u32[]{:S(2)}, u32[]{:S(2)}) async-start(f32[32,2,768]{2,1,0:T(2,128)} %reshape.83), calls=%async_computation.1 | async-start | bytes 393216 | tf_op jit(solution)/shard_map/all_to_all | solution.py:34
  39.8 2.9 %prep.1 = (f32[8,128]{1,0:T(8,128)}, f32[1,8960]{1,0:T(1,128)}, f32[1,6784]{1,0:T(1,128)}) custom-call(s32[1,6144]{1,0:T(1,128)} %bitcast.63, s32[48,128]{1,0:T(8,128)} %bitcast.64, s32[1,6144]{1,0:T(1,128)} %bitcast.65), custom_call_target="tpu_custom_call" | custom-call | tf_op jit(solution)/shard_map/prep/pallas_call | solution.py:110
  42.7 1.2 fusion.30.refs_0_.info_ref
  44.0 3.7 %all-to-all-done.1 = f32[32,2,768]{2,1,0:T(2,128)S(1)} async-done(((f32[32,2,768]{2,1,0:T(2,128)}), f32[32,2,768]{2,1,0:T(2,128)S(1)}, u32[]{:S(2)}, u32[]{:S(2)}) %all-to-all-start.1) | async-done | bytes 196640 | tf_op jit(solution)/shard_map/all_to_all | solution.py:34
  47.7 0.6 broadcast_in_dim.77
  48.4 10.0 %all-to-all-start.2 = ((bf16[8,2,768]{2,1,0:T(2,128)(2,1)}), bf16[8,2,768]{2,1,0:T(2,128)(2,1)S(1)}, u32[]{:S(2)}, u32[]{:S(2)}) async-start(bf16[8,2,768]{2,1,0:T(2,128)(2,1)} %broadcast_in_dim.77), calls=%async_computation.2 | async-start | bytes 49152 | tf_op jit(solution)/shard_map/all_to_all | solution.py:34
  58.4 1.3 collective-permute-start.5
  59.7 4.5 %collective-permute-start.4 = (bf16[8,400]{1,0:T(8,128)(2,1)S(1)}, bf16[8,400]{1,0:T(8,128)(2,1)S(1)}, u32[]{:S(2)}, u32[]{:S(2)}) collective-permute-start(bf16[8,400]{1,0:T(8,128)(2,1)S(1)} %get-tuple-element.55), channel_id=1, source_target_pairs={{0,1},{1,32},{32,33},{33,64},{64,65},{65,96},{96,97},{97,128},{128... | collective-permute-start | bytes 19208 | tf_op jit(solution)/shard_map/ppermute | solution.py:25
  64.2 2.0 %all-to-all-done.2.refs_1_ = bf16[8,2,768]{2,1,0:T(2,128)(2,1)S(1)} async-done(((bf16[8,2,768]{2,1,0:T(2,128)(2,1)}), bf16[8,2,768]{2,1,0:T(2,128)(2,1)S(1)}, u32[]{:S(2)}, u32[]{:S(2)}) %all-to-all-start.2) | async-done | bytes 24608 | tf_op jit(solution)/shard_map/all_to_all | solution.py:34
  66.2 0.6 copy-done.5
  66.8 1.6 windows.1
  68.4 4.9 %all-to-all-start.3 = ((bf16[32,2,640]{2,1,0:T(2,128)(2,1)}), bf16[32,2,640]{2,1,0:T(2,128)(2,1)S(1)}, u32[]{:S(2)}, u32[]{:S(2)}) async-start(bf16[32,2,640]{2,1,0:T(2,128)(2,1)} %windows.1), calls=%async_computation.3 | async-start | bytes 163840 | tf_op jit(solution)/shard_map/all_to_all | solution.py:34
  73.3 0.7 pad_maximum_fusion.target_ref
  74.4 0.7 reshape.87.fwd_ref
  75.1 0.7 reshape.88.back_ref
  75.8 0.7 copy-done.8
  76.5 0.7 copy.38.head_ref
  77.1 2.9 %all-to-all-done.3 = bf16[32,2,640]{2,1,0:T(2,128)(2,1)S(1)} async-done(((bf16[32,2,640]{2,1,0:T(2,128)(2,1)}), bf16[32,2,640]{2,1,0:T(2,128)(2,1)S(1)}, u32[]{:S(2)}, u32[]{:S(2)}) %all-to-all-start.3) | async-done | bytes 81952 | tf_op jit(solution)/shard_map/all_to_all | solution.py:34
  80.0 0.7 reshape.85.embed_ref
  80.7 25.0 %band.1 = (f32[128,384]{1,0:T(8,128)}, f32[32,2,768]{2,1,0:T(2,128)}) custom-call(s32[8]{0:T(128)} %fusion.30.refs_0_.info_ref, bf16[64,640]{1,0:T(8,128)(2,1)} %reshape.85.embed_ref, f32[1,8960]{1,0:T(1,128)} %get-tuple-element.29.flag_ref, f32[1,6784]{1,0:T(1,128)} %get-tuple-element.30.limit_ref, bf16[144,400]{1,0:T(8,128)(2,1)} %pad_maximum_fusion.target_ref, ...), custom_call_target="tpu_custom_call" | custom-call | tf_op jit(solution)/shard_map/band/pallas_call | solution.py:369
  105.6 13.4 %all_to_all.40.refs_1_ = f32[32,2,768]{2,1,0:T(2,128)} all-to-all(f32[32,2,768]{2,1,0:T(2,128)} %get-tuple-element.36), channel_id=1, replica_groups=mesh['enc'=8,'bin'=16,'off'=2] {'bin','off'}, dimensions={0} | all-to-all | bytes 393216 | tf_op jit(solution)/shard_map/all_to_all | solution.py:34
  119.1 1.8 %lines.1 = f32[8,2,1024]{2,1,0:T(2,128)} custom-call(s32[8]{0:T(128)} %fusion.30.refs_0_.info_ref, f32[32,2,768]{2,1,0:T(2,128)} %all_to_all.40.refs_1_), custom_call_target="tpu_custom_call" | custom-call | tf_op jit(solution)/shard_map/lines/pallas_call | solution.py:442
  120.9 13.7 %all_to_all.41 = f32[8,2,1024]{2,1,0:T(2,128)S(1)} all-to-all(f32[8,2,1024]{2,1,0:T(2,128)} %lines.1), channel_id=1, replica_groups=mesh['enc'=8,'bin'=16,'off'=2] {'enc'}, dimensions={0} | all-to-all | bytes 131072 | tf_op jit(solution)/shard_map/all_to_all | solution.py:34
  134.6 0.8 broadcast_in_dim.79
  135.4 5.0 %all-to-all-start.6 = ((f32[32,2,1024]{2,1,0:T(2,128)}), f32[32,2,1024]{2,1,0:T(2,128)S(1)}, u32[]{:S(2)}, u32[]{:S(2)}) async-start(f32[32,2,1024]{2,1,0:T(2,128)} %broadcast_in_dim.79), calls=%async_computation.6 | async-start | bytes 524288 | tf_op jit(solution)/shard_map/all_to_all | solution.py:34
  140.5 1.2 slice.71
  142.3 0.8 copy.41
  143.1 5.9 %all-to-all-done.6 = f32[32,2,1024]{2,1,0:T(2,128)S(1)} async-done(((f32[32,2,1024]{2,1,0:T(2,128)}), f32[32,2,1024]{2,1,0:T(2,128)S(1)}, u32[]{:S(2)}, u32[]{:S(2)}) %all-to-all-start.6) | async-done | bytes 262176 | tf_op jit(solution)/shard_map/all_to_all | solution.py:34
  151.2 0.7 pad_maximum_fusion.1
  151.9 3.4 %all-to-all-start.7 = ((f32[8,32,128]{2,1,0:T(8,128)}), f32[8,32,128]{2,1,0:T(8,128)S(1)}, u32[]{:S(2)}, u32[]{:S(2)}) async-start(f32[8,32,128]{2,1,0:T(8,128)} %pad_maximum_fusion.1), calls=%async_computation.7 | async-start | bytes 262144 | tf_op jit(solution)/shard_map/all_to_all | solution.py:34
  155.5 0.7 copy.39
  156.2 0.5 slice.82
  157.3 6.9 %all-to-all-done.7 = f32[8,32,128]{2,1,0:T(8,128)S(1)} async-done(((f32[8,32,128]{2,1,0:T(8,128)}), f32[8,32,128]{2,1,0:T(8,128)S(1)}, u32[]{:S(2)}, u32[]{:S(2)}) %all-to-all-start.7) | async-done | bytes 131104 | tf_op jit(solution)/shard_map/all_to_all | solution.py:34
  164.3 0.7 reshape.93
  164.9 0.7 reshape.94
  (60 shorter events, 4.7 us)
Async XLA Ops:
  0.6 32.4 %copy-start = (bf16[3,16,512]{2,1,0:T(8,128)(2,1)S(1)}, bf16[3,16,512]{2,1,0:T(8,128)(2,1)}, u32[]{:S(2)}) copy-start(bf16[3,16,512]{2,1,0:T(8,128)(2,1)} %param.12) | copy-start | bytes 147460
  1.6 5.8 %collective-permute-start.1 = (bf16[16,8]{1,0:T(8,128)(2,1)S(1)}, bf16[16,8]{1,0:T(8,128)(2,1)S(1)}, u32[]{:S(2)}, u32[]{:S(2)}) collective-permute-start(bf16[16,8]{1,0:T(8,128)(2,1)S(1)} %get-tuple-element.60), channel_id=1, source_target_pairs={{32,0},{64,32},{96,64},{128,96},{160,128},{192,160},{224,192},{33,... | collective-permute-start | bytes 776 | tf_op jit(solution)/shard_map/ppermute | solution.py:27
  2.9 5.9 %collective-permute-start = (bf16[16,8]{1,0:T(8,128)(2,1)S(1)}, bf16[16,8]{1,0:T(8,128)(2,1)S(1)}, u32[]{:S(2)}, u32[]{:S(2)}) collective-permute-start(bf16[16,8]{1,0:T(8,128)(2,1)S(1)} %get-tuple-element.59), channel_id=1, source_target_pairs={{0,32},{32,64},{64,96},{96,128},{128,160},{160,192},{192,224},{1,3... | collective-permute-start | bytes 776 | tf_op jit(solution)/shard_map/ppermute | solution.py:25
  9.8 7.8 %copy-start.3 = (bf16[384,128]{1,0:T(8,128)(2,1)S(1)}, bf16[384,128]{1,0:T(8,128)(2,1)}, u32[]{:S(2)}) copy-start(bf16[384,128]{1,0:T(8,128)(2,1)} %param.16) | copy-start | bytes 294916
  9.8 23.2 %all-to-all-start = ((bf16[32,16,784]{2,1,0:T(8,128)(2,1)}), bf16[32,16,784]{2,1,0:T(8,128)(2,1)S(1)}, u32[]{:S(2)}, u32[]{:S(2)}) async-start(bf16[32,16,784]{2,1,0:T(8,128)(2,1)} %broadcast_in_dim.67), calls=%async_computation | async-start | bytes 1835008 | tf_op jit(solution)/shard_map/all_to_all | solution.py:34
  17.7 10.6 %collective-permute-start.3 = (bf16[8,128]{0,1:T(8,128)(2,1)S(1)}, bf16[8,128]{0,1:T(8,128)(2,1)S(1)}, u32[]{:S(2)}, u32[]{:S(2)}) collective-permute-start(bf16[8,128]{0,1:T(8,128)(2,1)S(1)} %copy.33), channel_id=1, source_target_pairs={{2,0},{4,2},{6,4},{8,6},{10,8},{12,10},{14,12},{16,14},{18,16},{20... | collective-permute-start | bytes 6152 | tf_op jit(solution)/shard_map/ppermute | solution.py:27
  19.8 2.4 %copy-start.7 = (s32[2]{0:T(128)S(1)}, s32[2]{0:T(128)}, u32[]{:S(2)}) copy-start(s32[2]{0:T(128)} %param.19) | copy-start | bytes 28
  19.9 9.3 %collective-permute-start.2 = (bf16[8,128]{0,1:T(8,128)(2,1)S(1)}, bf16[8,128]{0,1:T(8,128)(2,1)S(1)}, u32[]{:S(2)}, u32[]{:S(2)}) collective-permute-start(bf16[8,128]{0,1:T(8,128)(2,1)S(1)} %copy.32), channel_id=1, source_target_pairs={{0,2},{2,4},{4,6},{6,8},{8,10},{10,12},{12,14},{14,16},{16,18},{18... | collective-permute-start | bytes 6152 | tf_op jit(solution)/shard_map/ppermute | solution.py:25
  24.2 0.7 copy-start.6
  33.0 0.7 copy-start.4
  34.9 12.7 %all-to-all-start.1 = ((f32[32,2,768]{2,1,0:T(2,128)}), f32[32,2,768]{2,1,0:T(2,128)S(1)}, u32[]{:S(2)}, u32[]{:S(2)}) async-start(f32[32,2,768]{2,1,0:T(2,128)} %reshape.83), calls=%async_computation.1 | async-start | bytes 393216 | tf_op jit(solution)/shard_map/all_to_all | solution.py:34
  48.4 17.9 %all-to-all-start.2 = ((bf16[8,2,768]{2,1,0:T(2,128)(2,1)}), bf16[8,2,768]{2,1,0:T(2,128)(2,1)S(1)}, u32[]{:S(2)}, u32[]{:S(2)}) async-start(bf16[8,2,768]{2,1,0:T(2,128)(2,1)} %broadcast_in_dim.77), calls=%async_computation.2 | async-start | bytes 49152 | tf_op jit(solution)/shard_map/all_to_all | solution.py:34
  58.4 14.9 %collective-permute-start.5 = (bf16[8,400]{1,0:T(8,128)(2,1)S(1)}, bf16[8,400]{1,0:T(8,128)(2,1)S(1)}, u32[]{:S(2)}, u32[]{:S(2)}) collective-permute-start(bf16[8,400]{1,0:T(8,128)(2,1)S(1)} %get-tuple-element.56), channel_id=1, source_target_pairs={{1,0},{32,1},{33,32},{64,33},{65,64},{96,65},{97,96},{128,97},{129... | collective-permute-start | bytes 19208 | tf_op jit(solution)/shard_map/ppermute | solution.py:27
  59.7 13.6 %collective-permute-start.4 = (bf16[8,400]{1,0:T(8,128)(2,1)S(1)}, bf16[8,400]{1,0:T(8,128)(2,1)S(1)}, u32[]{:S(2)}, u32[]{:S(2)}) collective-permute-start(bf16[8,400]{1,0:T(8,128)(2,1)S(1)} %get-tuple-element.55), channel_id=1, source_target_pairs={{0,1},{1,32},{32,33},{33,64},{64,65},{65,96},{96,97},{97,128},{128... | collective-permute-start | bytes 19208 | tf_op jit(solution)/shard_map/ppermute | solution.py:25
  66.2 0.6 copy-start.5
  68.4 11.6 %all-to-all-start.3 = ((bf16[32,2,640]{2,1,0:T(2,128)(2,1)}), bf16[32,2,640]{2,1,0:T(2,128)(2,1)S(1)}, u32[]{:S(2)}, u32[]{:S(2)}) async-start(bf16[32,2,640]{2,1,0:T(2,128)(2,1)} %windows.1), calls=%async_computation.3 | async-start | bytes 163840 | tf_op jit(solution)/shard_map/all_to_all | solution.py:34
  73.3 0.9 copy-start.1
  75.8 0.7 copy-start.8
  135.4 6.9 %copy-start.2 = (f32[128,384]{1,0:T(8,128)S(1)}, f32[128,384]{1,0:T(8,128)}, u32[]{:S(2)}) copy-start(f32[128,384]{1,0:T(8,128)} %get-tuple-element.35) | copy-start | bytes 589828
  135.4 13.6 %all-to-all-start.6 = ((f32[32,2,1024]{2,1,0:T(2,128)}), f32[32,2,1024]{2,1,0:T(2,128)S(1)}, u32[]{:S(2)}, u32[]{:S(2)}) async-start(f32[32,2,1024]{2,1,0:T(2,128)} %broadcast_in_dim.79), calls=%async_computation.6 | async-start | bytes 524288 | tf_op jit(solution)/shard_map/all_to_all | solution.py:34
  151.9 12.4 %all-to-all-start.7 = ((f32[8,32,128]{2,1,0:T(8,128)}), f32[8,32,128]{2,1,0:T(8,128)S(1)}, u32[]{:S(2)}, u32[]{:S(2)}) async-start(f32[8,32,128]{2,1,0:T(8,128)} %pad_maximum_fusion.1), calls=%async_computation.7 | async-start | bytes 262144 | tf_op jit(solution)/shard_map/all_to_all | solution.py:34
